TPU v7x, 32 devices: a whole 2x2x4 slice. The times are simulated.
32 devices in a mesh: rep: 4 (over x, y), dp: 8 (over z, core).
Axes of the slice: x: 2, y: 2, z: 4, core: 2. Of those that a mesh axis runs over, the one named last changes fastest.
Arguments:
- x: bfloat16 [32, 1024, 512], P(('rep', 'dp')), parts along dimension 0
- dy: bfloat16 [32, 1024, 512], P(('rep', 'dp')), parts along dimension 0
- w_gate: bfloat16 [2, 512, 8192], P(None, 'dp')
- w_up: bfloat16 [2, 512, 8192], P(None, 'dp')
- w_down: bfloat16 [2, 8192, 512], P(None, 'dp')
Outputs:
- output 1: bfloat16 [32, 1024, 512], P(('rep', 'dp')), parts along dimension 0
- output 2: bfloat16 [8, 512, 8192], P('rep', 'dp'), parts along dimension 0
- output 3: bfloat16 [8, 512, 8192], P('rep', 'dp'), parts along dimension 0
- output 4: bfloat16 [8, 8192, 512], P('rep', 'dp'), parts along dimension 0
There are 4 independent parts. A program takes and returns all parts, laid end to end along the dimension named above; an argument that names none is the same for every part.
All inputs are finite; a program needn't handle non-finite values.
Results may differ from a plain program's by a relative error of at most 0.018.
Values are sent between devices in bfloat16 or wider.
A program may use at most 2 GiB of HBM per device.

v0:
```python
import jax
import jax.numpy as jnp
from jax import lax

NAMES = ("w_gate", "w_up", "w_down")


def matmul(a, w):
    return jnp.dot(a, w, preferred_element_type=jnp.float32).astype(jnp.bfloat16)


def normed(h):
    wide = h.astype(jnp.float32)
    scale = lax.rsqrt(jnp.mean(wide**2, -1, keepdims=True) + 1e-6)
    return (wide * scale).astype(jnp.bfloat16)


def layer(h, w):
    a = normed(h)
    gate = jnp.dot(a, w["w_gate"], preferred_element_type=jnp.float32)
    up = jnp.dot(a, w["w_up"], preferred_element_type=jnp.float32)
    return h + matmul((jax.nn.silu(gate) * up).astype(jnp.bfloat16), w["w_down"])


def stack(weights, h):
    for number in range(weights["w_gate"].shape[0]):
        h = layer(h, {name: w[number] for name, w in weights.items()})
    return h


def solution(mesh):
    groups = mesh.shape["rep"]

    def step(x, dy, *weights):
        shape = x.shape
        x, dy = (t.reshape(groups, -1, *t.shape[1:]) for t in (x, dy))

        def of_a_group(x, dy):
            _, back = jax.vjp(stack, dict(zip(NAMES, weights, strict=True)), x)
            by_weights, by_x = back(dy)
            return (by_x, *(by_weights[name] for name in NAMES))

        by_x, *by_weights = jax.vmap(of_a_group)(x, dy)
        return (by_x.reshape(shape), *(t.reshape(-1, *t.shape[2:]) for t in by_weights))

    return step
```

profile of v0, /device:TPU:0, one launch (start us, length us, event | category | flops | bytes accessed | tf_op | source)
XLA Modules:
  0.0 1531.0 jit_solution(10838922329766808339)
XLA Ops:
  7.2 3.1 fusion.141
  10.4 3.0 fusion.140
  13.5 3.0 fusion.139
  19.9 74.9 %all-gather.30.cloned.1.call-done = bf16[1,512,8192]{2,1,0:T(8,128)(2,1)} async-done(((bf16[1,64,8192]{2,1,0:T(8,128)(2,1)}), bf16[1,512,8192]{2,1,0:T(8,128)(2,1)}) %all-gather.30.cloned.1.call-update) | async-done | bytes 8388624 | tf_op jit(solution)/vmap(jvp())/squeeze | solution.py:27
  94.7 18.0 %fusion.57 = f32[1024,8192]{1,0:T(8,128)} fusion(bf16[1,512,8192]{2,1,0:T(8,128)(2,1)} %all-gather.30.cloned.1.call-done, bf16[1,1024,512]{2,1,0:T(8,128)(2,1)S(1)} %copy-done.4, f32[1024]{0:T(1024)S(1)} %get-tuple-element.13), kind=kOutput, calls=%fused_computation.65 | convolution fusion | flops 8591507456 | bytes 42995712 | tf_op jit(solution)/vmap(jvp())/dot_general | solution.py:20
  112.8 64.5 %all-gather.32.cloned.1.call-done = bf16[1,512,8192]{2,1,0:T(8,128)(2,1)} async-done(((bf16[1,64,8192]{2,1,0:T(8,128)(2,1)}), bf16[1,512,8192]{2,1,0:T(8,128)(2,1)}) %all-gather.32.cloned.1.call-update) | async-done | bytes 8388624 | tf_op jit(solution)/vmap(jvp())/squeeze | solution.py:27
  177.3 17.9 %fusion.53 = f32[1024,8192]{1,0:T(8,128)} fusion(bf16[1,512,8192]{2,1,0:T(8,128)(2,1)} %all-gather.32.cloned.1.call-done, bf16[1,1024,512]{2,1,0:T(8,128)(2,1)S(1)} %copy-done.4, f32[1024]{0:T(1024)S(1)} %get-tuple-element.13), kind=kOutput, calls=%fused_computation.61 | convolution fusion | flops 8591507456 | bytes 42995712 | tf_op jit(solution)/vmap(jvp())/dot_general | solution.py:21
  195.2 27.4 %fusion.24 = bf16[1024,8192]{1,0:T(8,128)(2,1)} fusion(f32[1024,8192]{1,0:T(8,128)} %fusion.53, f32[1024,8192]{1,0:T(8,128)} %fusion.57), kind=kLoop, calls=%fused_computation.34 | loop fusion | flops 50331648 | bytes 83886080
  222.6 36.7 %all-gather.34.cloned.1.call-done = bf16[1,8192,512]{2,1,0:T(8,128)(2,1)} async-done(((bf16[1,1024,512]{2,1,0:T(8,128)(2,1)}), bf16[1,8192,512]{2,1,0:T(8,128)(2,1)}) %all-gather.34.cloned.1.call-update) | async-done | bytes 8388624 | tf_op jit(solution)/vmap(jvp())/squeeze | solution.py:27
  259.3 14.9 fusion.67
  274.9 66.8 %all-gather.36.cloned.1.call-done = bf16[1,512,8192]{2,1,0:T(8,128)(2,1)} async-done(((bf16[1,64,8192]{2,1,0:T(8,128)(2,1)}), bf16[1,512,8192]{2,1,0:T(8,128)(2,1)}) %all-gather.36.cloned.1.call-update) | async-done | bytes 8388624 | tf_op jit(solution)/vmap(jvp())/squeeze | solution.py:27
  341.7 19.0 %fusion.47 = f32[1024,8192]{1,0:T(8,128)} fusion(bf16[1,512,8192]{2,1,0:T(8,128)(2,1)} %all-gather.36.cloned.1.call-done, bf16[1,1,1024,512]{2,3,1,0:T(8,128)(2,1)S(1)} %get-tuple-element.15, f32[1024]{0:T(1024)S(1)} %bitcast.320), kind=kOutput, calls=%fused_computation.55 | convolution fusion | flops 8591507456 | bytes 42995712 | tf_op jit(solution)/vmap(jvp())/dot_general | solution.py:20
  360.6 63.4 %all-gather.40.cloned.1.call-done = bf16[1,512,8192]{2,1,0:T(8,128)(2,1)} async-done(((bf16[1,64,8192]{2,1,0:T(8,128)(2,1)}), bf16[1,512,8192]{2,1,0:T(8,128)(2,1)}) %all-gather.40.cloned.1.call-update) | async-done | bytes 8388624 | tf_op jit(solution)/vmap(jvp())/squeeze | solution.py:27
  424.0 18.7 %fusion.41 = f32[1024,8192]{1,0:T(8,128)} fusion(bf16[1,512,8192]{2,1,0:T(8,128)(2,1)} %all-gather.40.cloned.1.call-done, bf16[1,1,1024,512]{2,3,1,0:T(8,128)(2,1)S(1)} %get-tuple-element.15, f32[1024]{0:T(1024)S(1)} %bitcast.321), kind=kOutput, calls=%fused_computation.49 | convolution fusion | flops 8591507456 | bytes 42995712 | tf_op jit(solution)/vmap(jvp())/dot_general | solution.py:21
  442.7 29.4 %fusion.32 = f32[1,8192,512]{2,1,0:T(8,128)} fusion(f32[1024,8192]{1,0:T(8,128)} %fusion.41, f32[1024,8192]{1,0:T(8,128)} %fusion.47, bf16[1,1024,512]{2,1,0:T(8,128)(2,1)S(1)} %copy-done.12), kind=kOutput, calls=%fused_computation.43 | convolution fusion | flops 8640266240 | bytes 84934656 | tf_op jit(solution)/vmap(transpose(jvp()))/dot_general | solution.py:9
  472.9 32.9 %all-gather.38.cloned.1.call-done = bf16[1,8192,512]{2,1,0:T(8,128)(2,1)} async-done(((bf16[1,1024,512]{2,1,0:T(8,128)(2,1)}), bf16[1,8192,512]{2,1,0:T(8,128)(2,1)}) %all-gather.38.cloned.1.call-update) | async-done | bytes 8388624 | tf_op jit(solution)/vmap(jvp())/squeeze | solution.py:27
  505.9 15.1 convolution_convert_fusion.1
  521.0 27.0 %fusion.4 = bf16[1024,8192]{1,0:T(8,128)(2,1)S(1)} fusion(f32[1024,8192]{1,0:T(8,128)} %fusion.47, f32[1024,8192]{1,0:T(8,128)} %fusion.41, bf16[1024,8192]{1,0:T(8,128)(2,1)} %convolution_convert_fusion.1), kind=kLoop, calls=%fused_computation.10 | loop fusion | flops 100663296 | bytes 100663296
  548.0 5.7 copy-done
  553.8 12.3 fusion.76
  566.1 22.7 %fusion.69 = (f32[1024]{0:T(1024)S(1)}, bf16[1,1,1024,512]{2,3,1,0:T(8,128)(2,1)S(1)}) fusion(bf16[1,1,1024,512]{2,3,1,0:T(8,128)(2,1)S(1)} %get-tuple-element.15, bf16[1024,512]{0,1:T(8,128)(2,1)S(1)} %fusion.76, bf16[1,512,8192]{2,1,0:T(8,128)(2,1)} %all-gather.40.cloned.1.call-done, bf16[1024,8192]{1,0:T(8,128)(2,1)} %convolution_convert_fusion.1, ...), kind=kOutput, calls=%fused_computation.88 | convolution fusion | flops 8643410944 | bytes 61870080 | tf_op jit(solution)/vmap(transpose(jvp()))/dot_general | solution.py:21
  589.5 16.2 %convolution_bitcast_fusion = f32[1,8192,512]{2,1,0:T(8,128)} fusion(bf16[1024,8192]{1,0:T(8,128)(2,1)} %fusion.24, bf16[1,1,1024,512]{2,3,1,0:T(8,128)(2,1)S(1)} %fusion.119), kind=kOutput, calls=%fused_computation.46 | convolution fusion | flops 8589934592 | bytes 34603008 | tf_op jit(solution)/vmap(transpose(jvp()))/dot_general | solution.py:9
  605.8 25.6 %fusion.35 = f32[1,512,8192]{2,1,0:T(8,128)} fusion(bf16[1024,8192]{1,0:T(8,128)(2,1)} %convolution_convert_fusion.1, f32[1024,8192]{1,0:T(8,128)} %fusion.47, bf16[1,1,1024,512]{2,3,1,0:T(8,128)(2,1)S(1)} %get-tuple-element.15, f32[1024]{0:T(1024)S(1)} %bitcast.323), kind=kOutput, calls=%fused_computation.44 | convolution fusion | flops 8641839104 | bytes 68161536 | tf_op jit(solution)/vmap(transpose(jvp()))/dot_general | solution.py:21
  631.5 16.1 %convolution_convert_fusion = bf16[1024,8192]{1,0:T(8,128)(2,1)} fusion(bf16[1,8192,512]{2,1,0:T(8,128)(2,1)} %all-gather.34.cloned.1.call-done, bf16[1,1,1024,512]{2,3,1,0:T(8,128)(2,1)S(1)} %fusion.119), kind=kOutput, calls=%fused_computation.41 | convolution fusion | flops 8598323200 | bytes 26214400 | tf_op jit(solution)/vmap(transpose(jvp()))/dot_general | solution.py:9
  647.6 27.1 %fusion.7 = bf16[1024,8192]{1,0:T(8,128)(2,1)S(1)} fusion(f32[1024,8192]{1,0:T(8,128)} %fusion.57, f32[1024,8192]{1,0:T(8,128)} %fusion.53, bf16[1024,8192]{1,0:T(8,128)(2,1)} %convolution_convert_fusion), kind=kLoop, calls=%fused_computation.13 | loop fusion | flops 100663296 | bytes 100663296
  674.7 5.7 copy-done.1
  680.4 12.4 fusion.70
  692.8 22.1 %fusion.65 = (f32[1024]{0:T(1024)S(1)}, bf16[1,1,1024,512]{2,3,1,0:T(8,128)(2,1)}) fusion(bf16[1,1024,512]{1,2,0:T(8,128)(2,1)S(1)} %copy-done.6, bf16[1024,512]{0,1:T(8,128)(2,1)S(1)} %fusion.70, bf16[1,512,8192]{2,1,0:T(8,128)(2,1)} %all-gather.32.cloned.1.call-done, bf16[1024,8192]{1,0:T(8,128)(2,1)} %convolution_convert_fusion, f32[1024,8192]{1,0:T(8,128)} %fusion.57), kind=kOutput, calls=%fused_computation.84 | convolution fusion | flops 8643410944 | bytes 61870080 | tf_op jit(solution)/vmap(transpose(jvp()))/dot_general | solution.py:21
  715.0 25.6 %fusion.38 = f32[1,512,8192]{2,1,0:T(8,128)} fusion(bf16[1024,8192]{1,0:T(8,128)(2,1)} %convolution_convert_fusion, f32[1024,8192]{1,0:T(8,128)} %fusion.57, bf16[1,1024,512]{1,2,0:T(8,128)(2,1)S(1)} %copy-done.6, f32[1024]{0:T(1024)S(1)} %bitcast.329), kind=kOutput, calls=%fused_computation.45 | convolution fusion | flops 8641839104 | bytes 68161536 | tf_op jit(solution)/vmap(transpose(jvp()))/dot_general | solution.py:21
  741.8 15.7 %convolution_bitcast_fusion.2 = f32[1,512,8192]{2,1,0:T(8,128)} fusion(bf16[1024,8192]{1,0:T(8,128)(2,1)} %copy-done, bf16[1,1,1024,512]{2,3,1,0:T(8,128)(2,1)S(1)} %copy-done.3, f32[1024]{0:T(1024)S(1)} %bitcast.324), kind=kOutput, calls=%fused_computation.48 | convolution fusion | flops 8591507456 | bytes 34607104 | tf_op jit(solution)/vmap(transpose(jvp()))/dot_general | solution.py:20
  757.6 16.0 %convolution_bitcast_fusion.1 = f32[1,512,8192]{2,1,0:T(8,128)} fusion(bf16[1024,8192]{1,0:T(8,128)(2,1)} %copy-done.1, bf16[1,1024,512]{1,2,0:T(8,128)(2,1)S(1)} %copy-done.6, f32[1024]{0:T(1024)S(1)} %bitcast.330), kind=kOutput, calls=%fused_computation.47 | convolution fusion | flops 8591507456 | bytes 34607104 | tf_op jit(solution)/vmap(transpose(jvp()))/dot_general | solution.py:20
  773.6 1.2 copy-done.8
  774.8 1.9 fusion.118
  776.7 1.3 copy.2
  778.0 1.7 convert_bitcast_fusion.1
  779.7 64.5 %reduce-scatter.29.cloned.1.call-done = f32[1,1024,512]{2,1,0:T(8,128)} async-done(((f32[1,8192,512]{2,1,0:T(8,128)}), f32[1,1024,512]{2,1,0:T(8,128)}) %reduce-scatter.29.cloned.1.call-update) | async-done | bytes 2097168
  844.3 1.7 convert_bitcast_fusion
  846.0 1.5 add_bitcast_fusion
  847.5 166.0 %reduce-scatter.23.cloned.1.call-done = f32[1,64,8192]{2,1,0:T(8,128)} async-done(((f32[1,512,8192]{2,1,0:T(8,128)}), f32[1,64,8192]{2,1,0:T(8,128)}) %reduce-scatter.23.cloned.1.call-update) | async-done | bytes 2097168
  1013.4 1.7 convert_bitcast_fusion.3
  1015.1 167.3 %reduce-scatter.25.cloned.1.call-done = f32[1,64,8192]{2,1,0:T(8,128)} async-done(((f32[1,512,8192]{2,1,0:T(8,128)}), f32[1,64,8192]{2,1,0:T(8,128)}) %reduce-scatter.25.cloned.1.call-update) | async-done | bytes 2097168
  1182.4 1.7 convert_bitcast_fusion.2
  1184.1 1.5 add_bitcast_fusion.1
  1185.6 166.0 %reduce-scatter.19.cloned.1.call-done = f32[1,64,8192]{2,1,0:T(8,128)} async-done(((f32[1,512,8192]{2,1,0:T(8,128)}), f32[1,64,8192]{2,1,0:T(8,128)}) %reduce-scatter.19.cloned.1.call-update) | async-done | bytes 2097168
  1351.6 1.7 convert_bitcast_fusion.5
  1353.3 167.3 %reduce-scatter.21.cloned.1.call-done = f32[1,64,8192]{2,1,0:T(8,128)} async-done(((f32[1,512,8192]{2,1,0:T(8,128)}), f32[1,64,8192]{2,1,0:T(8,128)}) %reduce-scatter.21.cloned.1.call-update) | async-done | bytes 2097168
  1520.6 1.7 convert_bitcast_fusion.4
  1522.3 1.5 add_bitcast_fusion.2
  (63 shorter events, 7.0 us)
Async XLA Ops:
  7.2 11.2 copy-start.4
  7.2 87.6 %all-gather.30.cloned.1.call-start = ((), (), s32[]{:S(2)}) async-start(), calls=%async_computation.6 | async-start | bytes 9437184 | tf_op jit(solution)/vmap(jvp())/squeeze | solution.py:27
  10.4 166.9 %all-gather.32.cloned.1.call-start = ((), (), s32[]{:S(2)}) async-start(), calls=%async_computation.7 | async-start | bytes 9437184 | tf_op jit(solution)/vmap(jvp())/squeeze | solution.py:27
  13.5 245.8 %all-gather.34.cloned.1.call-start = ((), (), s32[]{:S(2)}) async-start(), calls=%async_computation.8 | async-start | bytes 9437184 | tf_op jit(solution)/vmap(jvp())/squeeze | solution.py:27
  16.6 325.1 %all-gather.36.cloned.1.call-start = ((), (), s32[]{:S(2)}) async-start(), calls=%async_computation.9 | async-start | bytes 9437184 | tf_op jit(solution)/vmap(jvp())/squeeze | solution.py:27
  17.2 406.9 %all-gather.40.cloned.1.call-start = ((), (), s32[]{:S(2)}) async-start(), calls=%async_computation.11 | async-start | bytes 9437184 | tf_op jit(solution)/vmap(jvp())/squeeze | solution.py:27
  17.8 488.1 %all-gather.38.cloned.1.call-start = ((), (), s32[]{:S(2)}) async-start(), calls=%async_computation.10 | async-start | bytes 9437184 | tf_op jit(solution)/vmap(jvp())/squeeze | solution.py:27
  18.3 759.7 %reduce-scatter.27.cloned.1.call-start = ((), (), s32[]{:S(2)}) async-start(), calls=%async_computation.16 | async-start | bytes 18874368
  19.2 240.0 %copy-start.5 = (bf16[1,1024,512]{1,2,0:T(8,128)(2,1)}, bf16[1,1024,512]{1,2,0:T(8,128)(2,1)S(1)}, u32[]{:S(2)}) copy-start(bf16[1,1024,512]{1,2,0:T(8,128)(2,1)S(1)} %copy.1) | copy-start | bytes 3145732
  274.2 331.6 %copy-start.2 = (bf16[1,1,1024,512]{2,3,1,0:T(8,128)(2,1)}, bf16[1,1,1024,512]{2,3,1,0:T(8,128)(2,1)S(1)}, u32[]{:S(2)}) copy-start(bf16[1,1,1024,512]{2,3,1,0:T(8,128)(2,1)S(1)} %get-tuple-element.15) | copy-start | bytes 3145732
  274.2 0.6 copy-start.13
  274.9 149.2 %copy-start.9 = (f32[1,1,1024]{2,1,0:T(1,128)}, f32[1,1,1024]{2,1,0:T(1,128)S(1)}, u32[]{:S(2)}) copy-start(f32[1,1,1024]{2,1,0:T(1,128)S(1)} %rsqrt.23) | copy-start | bytes 12292
  360.6 82.1 %copy-start.12 = (bf16[1,1024,512]{2,1,0:T(8,128)(2,1)S(1)}, bf16[1,1024,512]{2,1,0:T(8,128)(2,1)}, u32[]{:S(2)}) copy-start(bf16[1,1024,512]{2,1,0:T(8,128)(2,1)} %param) | copy-start | bytes 3145732
  472.1 372.1 %reduce-scatter.29.cloned.1.call-start = ((), (), s32[]{:S(2)}) async-start(), calls=%async_computation.17 | async-start | bytes 18874368
  548.0 5.7 copy-start
  566.1 22.7 %copy-start.14 = (f32[1024]{0:T(1024)S(1)}, f32[1024]{0:T(1024)}, u32[]{:S(2)}) copy-start(f32[1024]{0:T(1024)} %copy-done.13) | copy-start | bytes 12292
  566.1 22.7 %copy-start.10 = (f32[1,1,1024]{2,1,0:T(1,128)S(1)}, f32[1,1,1024]{2,1,0:T(1,128)}, u32[]{:S(2)}) copy-start(f32[1,1,1024]{2,1,0:T(1,128)} %copy-done.9) | copy-start | bytes 12292
  589.5 42.0 %copy-start.7 = (bf16[1,1,1024,512]{2,3,1,0:T(8,128)(2,1)}, bf16[1,1,1024,512]{2,3,1,0:T(8,128)(2,1)S(1)}, u32[]{:S(2)}) copy-start(bf16[1,1,1024,512]{2,3,1,0:T(8,128)(2,1)S(1)} %fusion.119) | copy-start | bytes 3145732
  605.8 407.7 %reduce-scatter.23.cloned.1.call-start = ((), (), s32[]{:S(2)}) async-start(), calls=%async_computation.14 | async-start | bytes 18874368
  631.5 551.0 %reduce-scatter.25.cloned.1.call-start = ((), (), s32[]{:S(2)}) async-start(), calls=%async_computation.15 | async-start | bytes 18874368
  674.7 5.7 copy-start.1
  680.4 12.4 copy-start.6
  692.8 22.1 %copy-start.15 = (f32[1024]{0:T(1024)S(1)}, f32[1024]{0:T(1024)}, u32[]{:S(2)}) copy-start(f32[1024]{0:T(1024)} %get-tuple-element.12) | copy-start | bytes 12292
  740.6 1.2 copy-start.3
  740.6 1.2 copy-start.11
  740.6 611.0 %reduce-scatter.19.cloned.1.call-start = ((), (), s32[]{:S(2)}) async-start(), calls=%async_computation.12 | async-start | bytes 18874368
  757.5 763.0 %reduce-scatter.21.cloned.1.call-start = ((), (), s32[]{:S(2)}) async-start(), calls=%async_computation.13 | async-start | bytes 18874368
  773.5 1.2 copy-start.8
Sparse Core Ops, SparseCore 0:
  10.5 84.1 all-gather.29
  96.9 80.3 all-gather.31
  178.9 80.3 all-gather.33
  261.3 80.3 all-gather.35
  343.7 80.3 all-gather.39
  425.5 80.3 all-gather.37
  508.2 166.8 reduce-scatter.26
  677.5 166.7 reduce-scatter.28
  846.6 166.7 reduce-scatter.22
  1015.6 166.7 reduce-scatter.24
  1184.8 166.7 reduce-scatter.18
  1353.8 166.7 reduce-scatter.20
where the time goes:
time: 1540 us; the launch traced here: 1530 us
  waiting for transfers between devices  1070 us (69%)
  matrix products  318 us (21%)
  other arithmetic  99.7 us (6%)
  local copies, waits for them, and re-layouts  26.3 us (2%)
    unnamed x18, waiting for transfers between devices  733 us
    squeeze x6, waiting for transfers between devices, stack(): h = layer(h, {name: w[number] for name, w in weights.items()})  339 us
    dot_general x6, matrix products, layer(): up = jnp.dot(a, w['w_up'], preferred_element_type=jnp.float32)  133 us
    dot_general x6, matrix products, layer(): gate = jnp.dot(a, w['w_gate'], preferred_element_type=jnp.float32)  93.3 us
    dot_general x5, matrix products, matmul(): jnp.dot(a, w, preferred_element_type=jnp.float32).astype(jnp.bfloat16)  91.7 us
    unnamed x3, other arithmetic  81.6 us
  transfers between devices with their start and end apart: 12, of which 11 were waited for; matrix products, arithmetic and copies ran while one was open for 28% of the time, Pallas kernels for 0%

commit v1 on v0

v1 whole, which is shorter than its diff:
```python
import functools

import jax
import jax.numpy as jnp
from jax import lax
from jax.sharding import PartitionSpec as P

F32, BF16 = jnp.float32, jnp.bfloat16


def normed(h):
    wide = h.astype(F32)
    scale = lax.rsqrt(jnp.mean(wide**2, -1, keepdims=True) + 1e-6)
    return (wide * scale).astype(BF16)


def dot(a, b, ca, cb):
    return lax.dot_general(a, b, (((ca,), (cb,)), ((), ())), preferred_element_type=F32)


def norm_back(h, da):
    wide = h.astype(F32)
    scale = lax.rsqrt(jnp.mean(wide**2, -1, keepdims=True) + 1e-6)
    da = da.astype(F32)
    inner = jnp.sum(da * wide, -1, keepdims=True)
    return (da * scale - wide * (scale**3 * inner / h.shape[-1])).astype(BF16)


def forward(h, a, wg, wu, wd):
    gate, up = dot(a, wg, 1, 0), dot(a, wu, 1, 0)
    p = (jax.nn.silu(gate) * up).astype(BF16)
    return h + dot(p, wd, 1, 0).astype(BF16)


def hidden_back(a, g, wg, wu, wd):
    gate, up = dot(a, wg, 1, 0), dot(a, wu, 1, 0)
    dp = dot(g, wd, 1, 1).astype(BF16).astype(F32)
    sig = jax.nn.sigmoid(gate)
    s = gate * sig
    p = (s * up).astype(BF16)
    dup = (dp * s).astype(BF16)
    dgate = (dp * up * (sig + s * (1 - sig))).astype(BF16)
    return p, dgate, dup


def back(h, a, g, wg, wu, wd):
    _, dgate, dup = hidden_back(a, g, wg, wu, wd)
    da = dot(dgate, wg, 1, 1).astype(BF16) + dot(dup, wu, 1, 1).astype(BF16)
    return g + norm_back(h, da)


def weights_back(a, g, wg, wu, wd):
    p, dgate, dup = hidden_back(a, g, wg, wu, wd)
    return dot(a, dgate, 0, 0).astype(BF16), dot(a, dup, 0, 0).astype(BF16), dot(p, g, 0, 0).astype(BF16)


def solution(mesh):
    layers = 2

    def body(x, dy, wg, wu, wd):
        gather = functools.partial(lax.all_gather, axis_name="dp", axis=0, tiled=True)
        me = lax.axis_index("dp")
        h, g = x[0], dy[0]
        width = wd.shape[1]
        full = [(gather(wg[n]), gather(wu[n]), gather(wd[n])) for n in range(layers)]
        own = [(lax.dynamic_slice_in_dim(f[0], me * width, width, 1), lax.dynamic_slice_in_dim(f[1], me * width, width, 1), wd[n])
               for n, f in enumerate(full)]
        hs, acts, all_a = [], [], []
        for n in range(layers):
            a = normed(h)
            hs.append(h)
            acts.append(a)
            all_a.append(gather(a))
            if n < layers - 1:
                h = forward(h, a, *full[n])
        grads = [None] * layers
        for n in reversed(range(layers)):
            all_g = gather(g)
            g = back(hs[n], acts[n], g, *full[n])
            bg, bu, bd = weights_back(all_a[n], all_g, *own[n])
            bg, bu = (lax.all_to_all(t, "dp", 0, 1, tiled=True) for t in (bg, bu))
            grads[n] = (bg, bu, bd)
        return (g[None], *(jnp.stack(t) for t in zip(*grads)))

    rows = P(("rep", "dp"), None, None)
    w = P(None, "dp", None)
    out = P("rep", "dp", None)
    return jax.shard_map(body, mesh=mesh, in_specs=(rows, rows, w, w, w), out_specs=(rows, out, out, out), check_vma=False)
```

time: 1540 us -> 1040 us (0.68)
  waiting for transfers between devices: 1070 us -> 471 us
  matrix products: 318 us -> 491 us
  other arithmetic: 99.7 us -> 11 us
  starting transfers between devices: 0.49 us -> 17.8 us
    unnamed x18 -> x10, waiting for transfers between devices: 733 us -> 2.38 us
    all_gather x0 -> x10, waiting for transfers between devices: none -> 460 us  [the longest x2 136 us: body(): gather(wu[n])]
    squeeze x6 -> x0, waiting for transfers between devices: 339 us -> none  [stack(): h = layer(h, {name: w[number] for name, w in weights.items()})]
    dot_general x17 -> x22, matrix products: 318 us -> 491 us  [dot(): lax.dot_general(a, b, (((ca,), (cb,)), ((), ())), preferred_element_type=...]
    unnamed x3 -> x0, other arithmetic: 81.6 us -> none
    all_to_all x0 -> x4, starting transfers between devices: none -> 17.4 us  [body(): bg, bu = (lax.all_to_all(t, 'dp', 0, 1, tiled=True) for t in (bg, bu))]
  transfers between devices with their start and end apart: 12 -> 14, of which waited for: 11 -> 10; matrix products, arithmetic and copies ran while one was open for 28% -> 50% of each run, Pallas kernels for 0% -> 0%
where the time goes in v1:
time: 1040 us; the launch traced here: 1030 us
  matrix products  491 us (47%)
  waiting for transfers between devices  471 us (45%)
  local copies, waits for them, and re-layouts  24.4 us (2%)
  starting transfers between devices  17.8 us (2%)
  between operations  15 us (1%)
  other arithmetic  11 us (1%)
    dot_general x22, matrix products, dot(): lax.dot_general(a, b, (((ca,), (cb,)), ((), ())), preferred_element_type=...  491 us
    all_gather x2, waiting for transfers between devices, body(): gather(wu[n])  136 us
    all_gather x2, waiting for transfers between devices, body(): gather(wg[n])  131 us
    all_gather x2, waiting for transfers between devices, body(): gather(wd[n])  119 us
    all_gather x2, waiting for transfers between devices, body(): all_a.append(gather(a))  60.5 us
  transfers between devices with their start and end apart: 14, of which 10 were waited for; matrix products, arithmetic and copies ran while one was open for 50% of the time, Pallas kernels for 0%

profile of v1, /device:TPU:0, one launch (start us, length us, event | category | flops | bytes accessed | tf_op | source)
XLA Modules:
  0.0 1030.1 jit_solution(15972897504344403102)
XLA Ops:
  7.2 3.2 fusion.164
  10.5 3.1 fusion.166
  13.7 3.0 fusion.165
  21.4 1.4 copy.9
  22.7 72.1 %all-gather.28.cloned.1.call-done = bf16[1,512,8192]{2,1,0:T(8,128)(2,1)} async-done(((bf16[1,64,8192]{2,1,0:T(8,128)(2,1)}), bf16[1,512,8192]{2,1,0:T(8,128)(2,1)}) %all-gather.28.cloned.1.call-update) | async-done | bytes 8388624 | tf_op jit(solution)/shard_map/all_gather | solution.py:65
  94.8 17.8 %fusion.48 = f32[1024,8192]{1,0:T(8,128)} fusion(bf16[1024,512]{0,1:T(8,128)(2,1)} %fusion.59, bf16[1,512,8192]{2,1,0:T(8,128)(2,1)} %all-gather.28.cloned.1.call-done), kind=kOutput, calls=%fused_computation.57 | convolution fusion | flops 8589934592 | bytes 42991616 | tf_op jit(solution)/shard_map/dot_general | solution.py:18
  112.6 64.1 %all-gather.26.cloned.1.call-done = bf16[1,512,8192]{2,1,0:T(8,128)(2,1)} async-done(((bf16[1,64,8192]{2,1,0:T(8,128)(2,1)}), bf16[1,512,8192]{2,1,0:T(8,128)(2,1)}) %all-gather.26.cloned.1.call-update) | async-done | bytes 8388624 | tf_op jit(solution)/shard_map/all_gather | solution.py:65
  176.8 18.7 %fusion.51 = f32[1024,8192]{1,0:T(8,128)} fusion(bf16[1024,512]{0,1:T(8,128)(2,1)S(1)} %copy-done.2, bf16[1,512,8192]{2,1,0:T(8,128)(2,1)} %all-gather.26.cloned.1.call-done), kind=kOutput, calls=%fused_computation.60 | convolution fusion | flops 8589934592 | bytes 42991616 | tf_op jit(solution)/shard_map/dot_general | solution.py:18
  195.5 63.8 %all-gather.30.cloned.1.call-done = bf16[1,8192,512]{2,1,0:T(8,128)(2,1)} async-done(((bf16[1,1024,512]{2,1,0:T(8,128)(2,1)}), bf16[1,8192,512]{2,1,0:T(8,128)(2,1)}) %all-gather.30.cloned.1.call-update) | async-done | bytes 8388624 | tf_op jit(solution)/shard_map/all_gather | solution.py:65
  259.3 26.2 %fusion.61 = (f32[1024]{0:T(1024)S(1)}, bf16[1024,512]{0,1:T(8,128)(2,1)S(1)}) fusion(bf16[1,8192,512]{2,1,0:T(8,128)(2,1)} %all-gather.30.cloned.1.call-done, f32[1024,8192]{1,0:T(8,128)} %fusion.48, f32[1024,8192]{1,0:T(8,128)} %fusion.51, bf16[1,1024,512]{1,2,0:T(8,128)(2,1)S(1)} %copy.10), kind=kOutput, calls=%fused_computation.80 | convolution fusion | flops 8642886656 | bytes 77598720 | tf_op jit(solution)/shard_map/dot_general | solution.py:18
  286.5 55.2 %all-gather.24.cloned.1.call-done = bf16[1,8192,512]{2,1,0:T(8,128)(2,1)} async-done(((bf16[1,1024,512]{2,1,0:T(8,128)(2,1)}), bf16[1,8192,512]{2,1,0:T(8,128)(2,1)}) %all-gather.24.cloned.1.call-update) | async-done | bytes 8388624 | tf_op jit(solution)/shard_map/all_gather | solution.py:65
  341.7 15.1 %convolution_convert_fusion.1 = bf16[1024,8192]{1,0:T(8,128)(2,1)} fusion(bf16[1,8192,512]{2,1,0:T(8,128)(2,1)} %all-gather.24.cloned.1.call-done, bf16[1,1024,512]{2,1,0:T(8,128)(2,1)S(1)} %copy-done.5), kind=kOutput, calls=%fused_computation.43 | convolution fusion | flops 8598323200 | bytes 26214400 | tf_op jit(solution)/shard_map/dot_general | solution.py:18
  356.9 66.7 %all-gather.34.cloned.1.call-done = bf16[1,512,8192]{2,1,0:T(8,128)(2,1)} async-done(((bf16[1,64,8192]{2,1,0:T(8,128)(2,1)}), bf16[1,512,8192]{2,1,0:T(8,128)(2,1)}) %all-gather.34.cloned.1.call-update) | async-done | bytes 8388624 | tf_op jit(solution)/shard_map/all_gather | solution.py:65
  423.6 18.9 %fusion.40 = f32[1024,8192]{1,0:T(8,128)} fusion(bf16[1024,512]{0,1:T(8,128)(2,1)S(1)} %fusion.62, bf16[1,512,8192]{2,1,0:T(8,128)(2,1)} %all-gather.34.cloned.1.call-done), kind=kOutput, calls=%fused_computation.50 | convolution fusion | flops 8589934592 | bytes 42991616 | tf_op jit(solution)/shard_map/dot_general | solution.py:18
  442.4 63.5 %all-gather.32.cloned.1.call-done = bf16[1,512,8192]{2,1,0:T(8,128)(2,1)} async-done(((bf16[1,64,8192]{2,1,0:T(8,128)(2,1)}), bf16[1,512,8192]{2,1,0:T(8,128)(2,1)}) %all-gather.32.cloned.1.call-update) | async-done | bytes 8388624 | tf_op jit(solution)/shard_map/all_gather | solution.py:65
  506.0 30.3 %fusion.75 = bf16[1024,512]{0,1:T(8,128)(2,1)} fusion(bf16[1,512,8192]{2,1,0:T(8,128)(2,1)} %all-gather.34.cloned.1.call-done, bf16[1024,8192]{1,0:T(8,128)(2,1)} %convolution_convert_fusion.1, f32[1024,8192]{1,0:T(8,128)} %fusion.40, bf16[1024,512]{0,1:T(8,128)(2,1)S(1)} %fusion.62, bf16[1,512,8192]{2,1,0:T(8,128)(2,1)} %all-gather.32.cloned.1.call-done), kind=kOutput, calls=%fused_computation.89 | convolution fusion | flops 17272668160 | bytes 69206016 | tf_op jit(solution)/shard_map/dot_general | solution.py:18
  536.3 24.4 %fusion.63 = (f32[1024]{0:T(1024)S(1)}, bf16[1024,512]{0,1:T(8,128)(2,1)}) fusion(bf16[1024,512]{0,1:T(8,128)(2,1)S(1)} %copy-done.10, bf16[1024,512]{0,1:T(8,128)(2,1)} %fusion.75, bf16[1,512,8192]{2,1,0:T(8,128)(2,1)} %all-gather.32.cloned.1.call-done, bf16[1024,8192]{1,0:T(8,128)(2,1)} %convolution_convert_fusion.1, f32[1024,8192]{1,0:T(8,128)} %fusion.40), kind=kOutput, calls=%fused_computation.82 | convolution fusion | flops 8651799552 | bytes 61870080 | tf_op jit(solution)/shard_map/dot_general | solution.py:18
  560.8 1.9 fusion.124
  562.7 16.3 %convolution_convert_fusion = bf16[1024,8192]{1,0:T(8,128)(2,1)} fusion(bf16[1024,512]{0,1:T(8,128)(2,1)S(1)} %fusion.124, bf16[1,8192,512]{2,1,0:T(8,128)(2,1)} %all-gather.30.cloned.1.call-done), kind=kOutput, calls=%fused_computation.42 | convolution fusion | flops 8598323200 | bytes 26214400 | tf_op jit(solution)/shard_map/dot_general | solution.py:18
  579.1 22.0 %fusion.87 = bf16[1024,512]{0,1:T(8,128)(2,1)} fusion(bf16[1,512,8192]{2,1,0:T(8,128)(2,1)} %all-gather.28.cloned.1.call-done, bf16[1024,8192]{1,0:T(8,128)(2,1)} %convolution_convert_fusion, f32[1024,8192]{1,0:T(8,128)} %fusion.51), kind=kOutput, calls=%fused_computation.91 | convolution fusion | flops 8649179136 | bytes 59768832 | tf_op jit(solution)/shard_map/dot_general | solution.py:18
  601.1 35.4 %fusion.60 = (f32[1024]{0:T(1024)S(1)}, bf16[1024,512]{0,1:T(8,128)(2,1)}) fusion(bf16[1,1024,512]{1,2,0:T(8,128)(2,1)S(1)} %copy-done.1, bf16[1024,512]{0,1:T(8,128)(2,1)} %fusion.87, bf16[1,512,8192]{2,1,0:T(8,128)(2,1)} %all-gather.26.cloned.1.call-done, f32[1024,8192]{1,0:T(8,128)} %fusion.48, bf16[1024,8192]{1,0:T(8,128)(2,1)} %convolution_convert_fusion, ...), kind=kOutput, calls=%fused_computation.79 | convolution fusion | flops 8685353984 | bytes 95424512 | tf_op jit(solution)/shard_map/dot_general | solution.py:18
  636.5 1.9 fusion.123
  639.8 17.8 %fusion.133 = f32[8192,1024]{1,0:T(8,128)} fusion(bf16[8192,512]{0,1:T(8,128)(2,1)} %all-gather.18.cloned.1.call-done, bf16[1,512,8192]{2,1,0:T(8,128)(2,1)} %all-gather.28.cloned.1.call-done, s32[]{:T(128)S(6)} %select_n.2), kind=kOutput, calls=%fused_computation.113 | convolution fusion | flops 8589934592 | bytes 42991620 | tf_op jit(solution)/shard_map/dot_general | solution.py:18
  657.6 18.0 %fusion.131 = f32[8192,1024]{1,0:T(8,128)} fusion(bf16[8192,512]{0,1:T(8,128)(2,1)} %all-gather.18.cloned.1.call-done, bf16[1,512,8192]{2,1,0:T(8,128)(2,1)} %all-gather.26.cloned.1.call-done, s32[]{:T(128)S(6)} %select_n.2), kind=kOutput, calls=%fused_computation.111 | convolution fusion | flops 8589934592 | bytes 42991620 | tf_op jit(solution)/shard_map/dot_general | solution.py:18
  675.7 16.3 %convolution_convert_fusion.2 = bf16[8192,1024]{1,0:T(8,128)(2,1)} fusion(bf16[1,8192,512]{2,1,0:T(8,128)(2,1)} %all-gather.36.cloned.1.call-done, bf16[2,1024,512]{2,1,0:T(8,128)(2,1)S(1)} %copy-done.11), kind=kOutput, calls=%fused_computation.44 | convolution fusion | flops 8598323200 | bytes 26214400 | tf_op jit(solution)/shard_map/dot_general | solution.py:18
  692.0 60.5 %all-gather.22.cloned.1.call-done = bf16[8192,512]{0,1:T(8,128)(2,1)} async-done(((bf16[1024,512]{0,1:T(8,128)(2,1)}), bf16[8192,512]{0,1:T(8,128)(2,1)}) %all-gather.22.cloned.1.call-update) | async-done | bytes 8388624 | tf_op jit(solution)/shard_map/all_gather | solution.py:73
  752.5 17.8 %fusion.128 = f32[8192,1024]{1,0:T(8,128)} fusion(bf16[8192,512]{0,1:T(8,128)(2,1)} %all-gather.22.cloned.1.call-done, bf16[1,512,8192]{2,1,0:T(8,128)(2,1)} %all-gather.32.cloned.1.call-done, s32[]{:T(128)S(6)} %select_n.2), kind=kOutput, calls=%fused_computation.108 | convolution fusion | flops 8589934592 | bytes 42991620 | tf_op jit(solution)/shard_map/dot_general | solution.py:18
  770.3 18.1 %fusion.126 = f32[8192,1024]{1,0:T(8,128)} fusion(bf16[8192,512]{0,1:T(8,128)(2,1)} %all-gather.22.cloned.1.call-done, bf16[1,512,8192]{2,1,0:T(8,128)(2,1)} %all-gather.34.cloned.1.call-done, s32[]{:T(128)S(6)} %select_n.2), kind=kOutput, calls=%fused_computation.106 | convolution fusion | flops 8589934592 | bytes 42991620 | tf_op jit(solution)/shard_map/dot_general | solution.py:18
  788.4 32.6 %fusion.67 = bf16[512,1024]{1,0:T(8,128)(2,1)} fusion(bf16[8192,512]{0,1:T(8,128)(2,1)} %all-gather.22.cloned.1.call-done, f32[8192,1024]{1,0:T(8,128)} %fusion.128, bf16[8192,1024]{1,0:T(8,128)(2,1)} %convolution_convert_fusion.2, f32[8192,1024]{1,0:T(8,128)} %fusion.126), kind=kOutput, calls=%fused_computation.87 | convolution fusion | flops 8682733568 | bytes 93323264 | tf_op jit(solution)/shard_map/dot_general | solution.py:18
  821.0 4.5 all-to-all-start.1
  825.5 14.1 %all-gather.20.cloned.1.call-done = bf16[8192,512]{0,1:T(8,128)(2,1)} async-done(((bf16[1024,512]{0,1:T(8,128)(2,1)}), bf16[8192,512]{0,1:T(8,128)(2,1)}) %all-gather.20.cloned.1.call-update) | async-done | bytes 8388624 | tf_op jit(solution)/shard_map/all_gather | solution.py:78
  839.6 16.0 %convolution_convert_fusion.3 = bf16[8192,1024]{1,0:T(8,128)(2,1)} fusion(bf16[8192,512]{0,1:T(8,128)(2,1)} %all-gather.20.cloned.1.call-done, bf16[2,1024,512]{2,1,0:T(8,128)(2,1)S(1)} %copy-done.11), kind=kOutput, calls=%fused_computation.45 | convolution fusion | flops 8598323200 | bytes 26214400 | tf_op jit(solution)/shard_map/dot_general | solution.py:18
  855.6 32.8 %fusion.64 = bf16[512,1024]{1,0:T(8,128)(2,1)} fusion(bf16[8192,512]{0,1:T(8,128)(2,1)} %all-gather.18.cloned.1.call-done, f32[8192,1024]{1,0:T(8,128)} %fusion.133, bf16[8192,1024]{1,0:T(8,128)(2,1)} %convolution_convert_fusion.3, f32[8192,1024]{1,0:T(8,128)} %fusion.131), kind=kOutput, calls=%fused_computation.86 | convolution fusion | flops 8682733568 | bytes 93323264 | tf_op jit(solution)/shard_map/dot_general | solution.py:18
  888.3 26.6 %fusion.105 = bf16[1,1024,512]{2,1,0:T(8,128)(2,1)} fusion(bf16[8192,512]{0,1:T(8,128)(2,1)} %all-gather.20.cloned.1.call-done, f32[8192,1024]{1,0:T(8,128)} %fusion.133, f32[8192,1024]{1,0:T(8,128)} %fusion.131), kind=kOutput, calls=%fused_computation.97 | convolution fusion | flops 8640790528 | bytes 76546048 | tf_op jit(solution)/shard_map/dot_general | solution.py:18
  914.9 5.5 all-to-all-start
  920.5 22.0 %fusion.95 = bf16[512,1024]{1,0:T(8,128)(2,1)} fusion(bf16[8192,512]{0,1:T(8,128)(2,1)} %all-gather.22.cloned.1.call-done, bf16[8192,1024]{1,0:T(8,128)(2,1)} %convolution_convert_fusion.2, f32[8192,1024]{1,0:T(8,128)} %fusion.126), kind=kOutput, calls=%fused_computation.93 | convolution fusion | flops 8649179136 | bytes 59768832 | tf_op jit(solution)/shard_map/dot_general | solution.py:18
  942.4 4.4 all-to-all-done
  946.8 3.6 all-to-all-start.3
  950.4 22.0 %fusion.92 = bf16[512,1024]{1,0:T(8,128)(2,1)} fusion(bf16[8192,512]{0,1:T(8,128)(2,1)} %all-gather.18.cloned.1.call-done, bf16[8192,1024]{1,0:T(8,128)(2,1)} %convolution_convert_fusion.3, f32[8192,1024]{1,0:T(8,128)} %fusion.131), kind=kOutput, calls=%fused_computation.92 | convolution fusion | flops 8649179136 | bytes 59768832 | tf_op jit(solution)/shard_map/dot_general | solution.py:18
  972.4 4.3 all-to-all-done.3
  976.8 3.8 all-to-all-start.2
  980.7 25.4 %fusion.106 = bf16[1,1024,512]{2,1,0:T(8,128)(2,1)S(1)} fusion(bf16[1,8192,512]{2,1,0:T(8,128)(2,1)} %all-gather.36.cloned.1.call-done, f32[8192,1024]{1,0:T(8,128)} %fusion.128, f32[8192,1024]{1,0:T(8,128)} %fusion.126), kind=kOutput, calls=%fused_computation.98 | convolution fusion | flops 8640790528 | bytes 76546048 | tf_op jit(solution)/shard_map/dot_general | solution.py:18
  1006.1 1.5 pad_maximum_fusion.2
  1007.6 2.8 copy.12
  1010.3 2.3 stack.28
  1012.7 1.5 copy.11
  1014.2 2.3 stack.27
  1018.8 3.9 pad_maximum_fusion
  (81 shorter events, 9.4 us)
Async XLA Ops:
  7.2 11.3 %copy-start.12 = (bf16[1,1024,512]{2,1,0:T(8,128)(2,1)S(1)}, bf16[1,1024,512]{2,1,0:T(8,128)(2,1)}, u32[]{:S(2)}) copy-start(bf16[1,1024,512]{2,1,0:T(8,128)(2,1)} %param.5) | copy-start | bytes 3145732
  7.2 14.2 %copy-start.5 = (bf16[1,1024,512]{2,1,0:T(8,128)(2,1)S(1)}, bf16[1,1024,512]{2,1,0:T(8,128)(2,1)}, u32[]{:S(2)}) copy-start(bf16[1,1024,512]{2,1,0:T(8,128)(2,1)} %param.6) | copy-start | bytes 3145732
  7.2 87.6 %all-gather.28.cloned.1.call-start = ((), (), s32[]{:S(2)}) async-start(), calls=%async_computation.9 | async-start | bytes 9437184 | tf_op jit(solution)/shard_map/all_gather | solution.py:65
  10.5 166.3 %all-gather.26.cloned.1.call-start = ((), (), s32[]{:S(2)}) async-start(), calls=%async_computation.8 | async-start | bytes 9437184 | tf_op jit(solution)/shard_map/all_gather | solution.py:65
  13.6 245.7 %all-gather.30.cloned.1.call-start = ((), (), s32[]{:S(2)}) async-start(), calls=%async_computation.10 | async-start | bytes 9437184 | tf_op jit(solution)/shard_map/all_gather | solution.py:65
  16.7 325.0 %all-gather.24.cloned.1.call-start = ((), (), s32[]{:S(2)}) async-start(), calls=%async_computation.7 | async-start | bytes 9437184 | tf_op jit(solution)/shard_map/all_gather | solution.py:65
  17.3 406.3 %all-gather.34.cloned.1.call-start = ((), (), s32[]{:S(2)}) async-start(), calls=%async_computation.12 | async-start | bytes 9437184 | tf_op jit(solution)/shard_map/all_gather | solution.py:65
  17.9 488.1 %all-gather.32.cloned.1.call-start = ((), (), s32[]{:S(2)}) async-start(), calls=%async_computation.11 | async-start | bytes 9437184 | tf_op jit(solution)/shard_map/all_gather | solution.py:65
  18.4 621.4 %all-gather.18.cloned.1.call-start = ((), (), s32[]{:S(2)}) async-start(), calls=%async_computation.4 | async-start | bytes 9437184 | tf_op jit(solution)/shard_map/all_gather | solution.py:73
  19.0 240.3 %copy-start = (bf16[1,1024,512]{1,2,0:T(8,128)(2,1)}, bf16[1,1024,512]{1,2,0:T(8,128)(2,1)S(1)}, u32[]{:S(2)}) copy-start(bf16[1,1024,512]{1,2,0:T(8,128)(2,1)S(1)} %copy.10) | copy-start | bytes 3145732
  19.3 3.4 copy-start.14
  19.3 3.4 copy-start.16
  20.6 655.1 %all-gather.36.cloned.1.call-start = ((), (), s32[]{:S(2)}) async-start(), calls=%async_computation.13 | async-start | bytes 9437184 | tf_op jit(solution)/shard_map/all_gather | solution.py:78
  21.3 731.1 %all-gather.22.cloned.1.call-start = ((), (), s32[]{:S(2)}) async-start(), calls=%async_computation.6 | async-start | bytes 9437184 | tf_op jit(solution)/shard_map/all_gather | solution.py:73
  22.7 154.1 %copy-start.2 = (bf16[1024,512]{0,1:T(8,128)(2,1)S(1)}, bf16[1024,512]{0,1:T(8,128)(2,1)}, u32[]{:S(2)}) copy-start(bf16[1024,512]{0,1:T(8,128)(2,1)} %fusion.59) | copy-start | bytes 3145732
  285.6 71.3 %copy-start.9 = (bf16[1024,512]{0,1:T(8,128)(2,1)}, bf16[1024,512]{0,1:T(8,128)(2,1)S(1)}, u32[]{:S(2)}) copy-start(bf16[1024,512]{0,1:T(8,128)(2,1)S(1)} %get-tuple-element.15) | copy-start | bytes 3145732
  285.6 220.4 %copy-start.20 = (f32[1024]{0:T(1024)}, f32[1024]{0:T(1024)S(1)}, u32[]{:S(2)}) copy-start(f32[1024]{0:T(1024)S(1)} %get-tuple-element.14) | copy-start | bytes 12292
  285.6 0.6 copy-start.18
  286.5 219.4 %copy-start.4 = (bf16[1024,512]{0,1:T(8,128)(2,1)}, bf16[1024,512]{0,1:T(8,128)(2,1)S(1)}, u32[]{:S(2)}) copy-start(bf16[1024,512]{0,1:T(8,128)(2,1)S(1)} %fusion.62) | copy-start | bytes 3145732
  442.4 93.8 %copy-start.10 = (bf16[1024,512]{0,1:T(8,128)(2,1)S(1)}, bf16[1024,512]{0,1:T(8,128)(2,1)}, u32[]{:S(2)}) copy-start(bf16[1024,512]{0,1:T(8,128)(2,1)} %copy-done.9) | copy-start | bytes 3145732
  536.3 24.5 %copy-start.21 = (f32[1024]{0:T(1024)S(1)}, f32[1024]{0:T(1024)}, u32[]{:S(2)}) copy-start(f32[1024]{0:T(1024)} %copy-done.20) | copy-start | bytes 12292
  536.3 24.5 %copy-start.8 = (bf16[1,1024,512]{1,2,0:T(8,128)(2,1)S(1)}, bf16[1,1024,512]{1,2,0:T(8,128)(2,1)}, u32[]{:S(2)}) copy-start(bf16[1,1024,512]{1,2,0:T(8,128)(2,1)} %copy.9) | copy-start | bytes 3145732
  536.3 24.5 %copy-start.19 = (f32[1024]{0:T(1024)S(1)}, f32[1024]{0:T(1024)}, u32[]{:S(2)}) copy-start(f32[1024]{0:T(1024)} %copy-done.18) | copy-start | bytes 12292
  560.7 278.9 %all-gather.20.cloned.1.call-start = ((), (), s32[]{:S(2)}) async-start(), calls=%async_computation.5 | async-start | bytes 9437184 | tf_op jit(solution)/shard_map/all_gather | solution.py:78
  562.7 73.8 %copy-start.3 = (bf16[1024,512]{0,1:T(8,128)(2,1)}, bf16[1024,512]{0,1:T(8,128)(2,1)S(1)}, u32[]{:S(2)}) copy-start(bf16[1024,512]{0,1:T(8,128)(2,1)S(1)} %fusion.124) | copy-start | bytes 3145732
  579.1 22.0 %copy-start.1 = (bf16[1,1024,512]{1,2,0:T(8,128)(2,1)S(1)}, bf16[1,1024,512]{1,2,0:T(8,128)(2,1)}, u32[]{:S(2)}) copy-start(bf16[1,1024,512]{1,2,0:T(8,128)(2,1)} %copy-done) | copy-start | bytes 3145732
  601.0 35.4 %copy-start.15 = (f32[1024]{0:T(1024)S(1)}, f32[1024]{0:T(1024)}, u32[]{:S(2)}) copy-start(f32[1024]{0:T(1024)} %copy-done.14) | copy-start | bytes 12292
  601.0 35.4 %copy-start.17 = (f32[1024]{0:T(1024)S(1)}, f32[1024]{0:T(1024)}, u32[]{:S(2)}) copy-start(f32[1024]{0:T(1024)} %copy-done.16) | copy-start | bytes 12292
  657.6 18.0 %copy-start.11 = (bf16[2,1024,512]{2,1,0:T(8,128)(2,1)S(1)}, bf16[2,1024,512]{2,1,0:T(8,128)(2,1)}, u32[]{:S(2)}) copy-start(bf16[2,1024,512]{2,1,0:T(8,128)(2,1)} %param.9) | copy-start | bytes 6291460
  821.0 93.9 %all-to-all-start.1 = ((bf16[8,64,1024]{2,1,0:T(8,128)(2,1)}), bf16[8,64,1024]{2,1,0:T(8,128)(2,1)}, u32[]{:S(2)}, u32[]{:S(2)}) async-start(bf16[8,64,1024]{2,1,0:T(8,128)(2,1)} %bitcast.18), calls=%async_computation.1 | async-start | bytes 2097152 | tf_op jit(solution)/shard_map/all_to_all | solution.py:81
  914.9 31.9 %all-to-all-start = ((bf16[8,64,1024]{2,1,0:T(8,128)(2,1)}), bf16[8,64,1024]{2,1,0:T(8,128)(2,1)S(1)}, u32[]{:S(2)}, u32[]{:S(2)}) async-start(bf16[8,64,1024]{2,1,0:T(8,128)(2,1)} %bitcast.12), calls=%async_computation | async-start | bytes 2097152 | tf_op jit(solution)/shard_map/all_to_all | solution.py:81
  946.8 25.6 %copy-start.6 = (bf16[8,64,1024]{2,1,0:T(8,128)(2,1)}, bf16[8,64,1024]{2,1,0:T(8,128)(2,1)S(1)}, u32[]{:S(2)}) copy-start(bf16[8,64,1024]{2,1,0:T(8,128)(2,1)S(1)} %all-to-all-done) | copy-start | bytes 3145732
  946.8 29.9 %all-to-all-start.3 = ((bf16[8,64,1024]{2,1,0:T(8,128)(2,1)}), bf16[8,64,1024]{2,1,0:T(8,128)(2,1)S(1)}, u32[]{:S(2)}, u32[]{:S(2)}) async-start(bf16[8,64,1024]{2,1,0:T(8,128)(2,1)} %bitcast.22), calls=%async_computation.3 | async-start | bytes 2097152 | tf_op jit(solution)/shard_map/all_to_all | solution.py:81
  976.8 40.9 %all-to-all-start.2 = ((bf16[8,64,1024]{2,1,0:T(8,128)(2,1)}), bf16[8,64,1024]{2,1,0:T(8,128)(2,1)S(1)}, u32[]{:S(2)}, u32[]{:S(2)}) async-start(bf16[8,64,1024]{2,1,0:T(8,128)(2,1)} %bitcast.123), calls=%async_computation.2 | async-start | bytes 2097152 | tf_op jit(solution)/shard_map/all_to_all | solution.py:81
  980.6 25.4 %copy-start.13 = (bf16[1,1024,512]{2,1,0:T(8,128)(2,1)S(1)}, bf16[1,1024,512]{2,1,0:T(8,128)(2,1)}, u32[]{:S(2)}) copy-start(bf16[1,1024,512]{2,1,0:T(8,128)(2,1)} %fusion.105) | copy-start | bytes 3145732
  980.6 32.0 %copy-start.7 = (bf16[8,64,1024]{2,1,0:T(8,128)(2,1)S(1)}, bf16[8,64,1024]{2,1,0:T(8,128)(2,1)}, u32[]{:S(2)}) copy-start(bf16[8,64,1024]{2,1,0:T(8,128)(2,1)} %copy-done.6) | copy-start | bytes 3145732
Sparse Core Ops, SparseCore 0:
  10.6 84.1 all-gather.27
  96.4 80.3 all-gather.25
  179.0 80.3 all-gather.29
  261.4 80.3 all-gather.23
  343.2 80.3 all-gather.33
  425.6 80.3 all-gather.31
  508.1 80.3 all-gather.17
  590.1 80.3 all-gather.35
  672.1 80.3 all-gather.21
  754.5 85.1 all-gather.19

commit v2 on v1

v2 whole, which is shorter than its diff:
```python
import functools

import jax
import jax.numpy as jnp
from jax import lax
from jax.experimental import pallas as pl
from jax.experimental.pallas import tpu as pltpu
from jax.sharding import PartitionSpec as P

F32, BF16 = jnp.float32, jnp.bfloat16


def normed(h):
    wide = h.astype(F32)
    scale = lax.rsqrt(jnp.mean(wide**2, -1, keepdims=True) + 1e-6)
    return (wide * scale).astype(BF16)


def dot(a, b, ca, cb):
    return lax.dot_general(a, b, (((ca,), (cb,)), ((), ())), preferred_element_type=F32)


def norm_back(h, da):
    wide = h.astype(F32)
    scale = lax.rsqrt(jnp.mean(wide**2, -1, keepdims=True) + 1e-6)
    da = da.astype(F32)
    inner = jnp.sum(da * wide, -1, keepdims=True)
    return (da * scale - wide * (scale**3 * inner / h.shape[-1])).astype(BF16)


def hidden_back(gate, up, dp):
    dp = dp.astype(BF16).astype(F32)
    sig = jax.nn.sigmoid(gate)
    s = gate * sig
    return (s * up).astype(BF16), (dp * up * (sig + s * (1 - sig))).astype(BF16), (dp * s).astype(BF16)


ROWS = 256


def forward_kernel(h_ref, wg_ref, wu_ref, wd_ref, out_ref, normed_ref, a_ref, acc_ref):
    step = pl.program_id(0)

    @pl.when(step == 0)
    def _():
        a_ref[...] = normed(h_ref[...])
        acc_ref[...] = jnp.zeros_like(acc_ref)

    for r in range(0, h_ref.shape[0], ROWS):
        rows = pl.ds(r, ROWS)
        a = a_ref[rows, :]
        gate, up = dot(a, wg_ref[...], 1, 0), dot(a, wu_ref[...], 1, 0)
        p = (gate * jax.nn.sigmoid(gate) * up).astype(BF16)
        acc_ref[rows, :] += dot(p, wd_ref[...], 1, 0)

    @pl.when(step == pl.num_programs(0) - 1)
    def _():
        h = h_ref[...] + acc_ref[...].astype(BF16)
        out_ref[...] = h
        normed_ref[...] = normed(h)


def forward(h, wg, wu, wd, width=1024):
    tokens, d = h.shape
    ff = wd.shape[0]
    whole = pl.BlockSpec((tokens, d), lambda k: (0, 0))
    column = pl.BlockSpec((d, width), lambda k: (0, k))
    return pl.pallas_call(
        forward_kernel,
        grid=(ff // width,),
        in_specs=[whole, column, column, pl.BlockSpec((width, d), lambda k: (k, 0))],
        out_specs=[whole, whole],
        out_shape=[jax.ShapeDtypeStruct(h.shape, BF16)] * 2,
        scratch_shapes=[pltpu.VMEM((tokens, d), BF16), pltpu.VMEM((tokens, d), F32)],
        cost_estimate=pl.CostEstimate(flops=6 * tokens * d * ff, bytes_accessed=6 * d * ff, transcendentals=tokens * ff),
        name="forward",
    )(h, wg, wu, wd)


def back_kernel(h_ref, g_ref, wg_ref, wu_ref, wd_ref, out_ref, a_ref, accg_ref, accu_ref):
    step = pl.program_id(0)

    @pl.when(step == 0)
    def _():
        a_ref[...] = normed(h_ref[...])
        accg_ref[...] = jnp.zeros_like(accg_ref)
        accu_ref[...] = jnp.zeros_like(accu_ref)

    for r in range(0, h_ref.shape[0], ROWS):
        rows = pl.ds(r, ROWS)
        a = a_ref[rows, :]
        gate, up = dot(a, wg_ref[...], 1, 0), dot(a, wu_ref[...], 1, 0)
        _, dgate, dup = hidden_back(gate, up, dot(g_ref[rows, :], wd_ref[...], 1, 1))
        accg_ref[rows, :] += dot(dgate, wg_ref[...], 1, 1)
        accu_ref[rows, :] += dot(dup, wu_ref[...], 1, 1)

    @pl.when(step == pl.num_programs(0) - 1)
    def _():
        da = accg_ref[...].astype(BF16) + accu_ref[...].astype(BF16)
        out_ref[...] = g_ref[...] + norm_back(h_ref[...], da)


def back(h, g, wg, wu, wd, width=1024):
    tokens, d = h.shape
    ff = wd.shape[0]
    whole = pl.BlockSpec((tokens, d), lambda k: (0, 0))
    column = pl.BlockSpec((d, width), lambda k: (0, k))
    return pl.pallas_call(
        back_kernel,
        grid=(ff // width,),
        in_specs=[whole, whole, column, column, pl.BlockSpec((width, d), lambda k: (k, 0))],
        out_specs=whole,
        out_shape=jax.ShapeDtypeStruct(h.shape, BF16),
        scratch_shapes=[pltpu.VMEM((tokens, d), BF16), pltpu.VMEM((tokens, d), F32), pltpu.VMEM((tokens, d), F32)],
        cost_estimate=pl.CostEstimate(flops=10 * tokens * d * ff, bytes_accessed=6 * d * ff, transcendentals=tokens * ff),
        name="back",
    )(h, g, wg, wu, wd)


GROUP = 8


def weights_kernel(a_ref, g_ref, wg_ref, wu_ref, wd_ref, bg_ref, bu_ref, bd_ref, accg_ref, accu_ref, accd_ref, stageg_ref, stageu_ref,
                   kept, sends, receives):
    chunk, step = pl.program_id(0), pl.program_id(1)
    chunks, steps = pl.num_programs(0), pl.num_programs(1)
    tokens, width = a_ref.shape[0], wg_ref.shape[1]
    height = bg_ref.shape[0]
    rep, me = lax.axis_index("rep"), lax.axis_index("dp")
    barrier = pltpu.get_barrier_semaphore()

    @pl.when((chunk == 0) & (step == 0))
    def _():
        for j in range(1, GROUP):
            pl.semaphore_signal(barrier, inc=1, device_id=(rep, lax.rem(me + j, GROUP)), device_id_type=pl.DeviceIdType.MESH)

    @pl.when(step == 0)
    def _():
        for acc in (accg_ref, accu_ref, accd_ref):
            acc[...] = jnp.zeros_like(acc)

    ps, dgs, dus = [], [], []
    for r in range(0, tokens, ROWS):
        rows = pl.ds(r, ROWS)
        a, g = a_ref[rows, :], g_ref[rows, :]
        gate, up = dot(a, wg_ref[...], 1, 0), dot(a, wu_ref[...], 1, 0)
        p, dgate, dup = hidden_back(gate, up, dot(g, wd_ref[...], 1, 1))
        ps.append(p), dgs.append(dgate), dus.append(dup)
    p, dgate, dup = (jnp.concatenate(t, 0) for t in (ps, dgs, dus))
    accg_ref[...] += dot(a_ref[...], dgate, 0, 0)
    accu_ref[...] += dot(a_ref[...], dup, 0, 0)
    accd_ref[...] += dot(p, g_ref[...], 0, 0)

    pairs = ((stageg_ref, bg_ref), (stageu_ref, bu_ref))

    def to_own(c, m):
        stage, out = pairs[m]
        columns = pl.ds(pl.multiple_of((me * chunks + c) * width, width), width)
        return pltpu.make_async_copy(stage.at[c, pl.ds(pl.multiple_of(me * height, height), height)], out.at[:, columns], kept.at[c, m])

    def to_peer(c, m, j):
        stage, out = pairs[m]
        columns = pl.ds(pl.multiple_of((me * chunks + c) * width, width), width)
        peer = lax.rem(me + j, GROUP)
        return pltpu.make_async_remote_copy(
            src_ref=stage.at[c, pl.ds(pl.multiple_of(peer * height, height), height)], dst_ref=out.at[:, columns],
            send_sem=sends.at[c, m, j - 1], recv_sem=receives.at[c, m, j - 1], device_id=(rep, peer), device_id_type=pl.DeviceIdType.MESH)

    @pl.when((chunk == 0) & (step == steps - 1))
    def _():
        pl.semaphore_wait(barrier, GROUP - 1)

    @pl.when(step == steps - 1)
    def _():
        for m, acc in ((0, accg_ref), (1, accu_ref)):
            pairs[m][0][chunk] = acc[...].astype(BF16)
            for j in (4, 3, 5, 2, 6, 1, 7):
                to_peer(chunk, m, j).start()
            to_own(chunk, m).start()
        bd_ref[...] = accd_ref[...].astype(BF16)

    @pl.when((chunk == chunks - 1) & (step == steps - 1))
    def _():
        def finish(c, _):
            for m in range(2):
                to_own(c, m).wait()
                for j in range(1, GROUP):
                    to_peer(c, m, j).wait()
            return 0

        lax.fori_loop(0, chunks, finish, 0)


def weights_back(a, g, wg, wu, wd, collective_id, width=256, block=1024):
    tokens, d = a.shape
    ff = wd.shape[0]
    chunks = ff // width
    rows = pl.BlockSpec((block, d), lambda k, t: (t, 0))
    column = pl.BlockSpec((d, width), lambda k, t: (0, k))
    down = pl.BlockSpec((width, d), lambda k, t: (k, 0))
    anywhere = pl.BlockSpec(memory_space=pltpu.HBM)
    spread = jax.ShapeDtypeStruct((d // GROUP, ff * GROUP), BF16)
    dma = pltpu.SemaphoreType.DMA
    return pl.pallas_call(
        weights_kernel,
        grid=(chunks, tokens // block),
        in_specs=[rows, rows, column, column, down],
        out_specs=[anywhere, anywhere, down],
        out_shape=[spread, spread, jax.ShapeDtypeStruct((ff, d), BF16)],
        scratch_shapes=[pltpu.VMEM((d, width), F32), pltpu.VMEM((d, width), F32), pltpu.VMEM((width, d), F32),
                        pltpu.VMEM((chunks, d, width), BF16), pltpu.VMEM((chunks, d, width), BF16),
                        dma((chunks, 2)), dma((chunks, 2, GROUP - 1)), dma((chunks, 2, GROUP - 1))],
        compiler_params=pltpu.CompilerParams(collective_id=collective_id, has_side_effects=True),
        cost_estimate=pl.CostEstimate(flops=12 * tokens * d * ff, bytes_accessed=4 * d * tokens * chunks, transcendentals=tokens * ff),
        name="weights_back",
    )(a, g, wg, wu, wd)


MESH = pl.DeviceIdType.MESH


class Gather:
    def __init__(self, n, own, out, stage, load, store, zs, zr, hs, ps, pr, fs, fr, cs, cr):
        self.n, self.own, self.out, self.stage = n, own, out, stage
        self.load, self.store = load, store
        self.zs, self.zr, self.hs, self.ps, self.pr, self.fs, self.fr, self.cs, self.cr = zs, zr, hs, ps, pr, fs, fr, cs, cr
        rep, dp = lax.axis_index("rep"), lax.axis_index("dp")
        z, core = dp // 2, lax.rem(dp, 2)
        self.rep, self.dp, self.z, self.core = rep, dp, z, core
        self.inner = lax.rem((z + 1) // 2, 2)
        self.high = z // 2
        self.over_x = lax.rem(rep + 2, 4)
        self.over_y = rep + 1 - 2 * lax.rem(rep, 2)
        self.across = 3 - rep
        self.to_x, self.to_y, self.to_core = (self.over_x, dp), (self.over_y, dp), (rep, z * 2 + 1 - core)
        self.sent, self.handed = [], []

    def along(self, z):
        return (self.rep, z * 2 + self.core)

    def source(self, k):
        low = (1 - self.z, 2, 3)[k]
        high = (5 - self.z, 1, 0)[k]
        return self.high * high + (1 - self.high) * low

    def barrier(self):
        semaphore = pltpu.get_barrier_semaphore()
        peers = [self.along(lax.rem(self.z + j, 4)) for j in (1, 2, 3)] + [self.to_x, self.to_y, self.to_core]
        for peer in peers:
            pl.semaphore_signal(semaphore, inc=1, device_id=peer, device_id_type=MESH)
        pl.semaphore_wait(semaphore, len(peers))

    def rows(self, i, z, core, quarter=None):
        size = self.own[i].shape[0]
        start = (z * 2 + core) * size
        if quarter is None:
            return self.out[i].at[pl.ds(pl.multiple_of(start, size), size)]
        part = size // 4
        return self.out[i].at[pl.ds(pl.multiple_of(start + quarter * part, part), part)]

    def copy(self, src, dst, send, receive, peer):
        return pltpu.make_async_remote_copy(src_ref=src, dst_ref=dst, send_sem=send, recv_sem=receive, device_id=peer, device_id_type=MESH)

    def start(self, *args):
        copy = self.copy(*args)
        copy.start()
        self.sent.append(copy)

    def begin(self, i):
        part = self.own[i].shape[0] // 4
        mine = self.own[i].at[pl.ds(pl.multiple_of(self.rep * part, part), part)]
        there = self.rows(i, self.z, self.core, self.rep)
        inner = self.inner
        outward = inner * (3 * self.z - 3) + (1 - inner) * (2 - self.z // 3)
        self.start(mine, there, self.zs.at[2 * i], self.zr.at[3 * i + inner], self.along(1 + lax.rem(self.z, 2)))
        self.start(mine, there, self.zs.at[2 * i + 1], self.zr.at[3 * i + 2 * (1 - inner)], self.along(outward))
        self.start(self.own[i], self.rows(i, self.z, self.core), self.cs.at[4 * i], self.cr.at[4 * i], self.to_core)
        self.local(i, 0).start()

    def local(self, i, leg):
        if leg == 0:
            return pltpu.make_async_copy(self.own[i], self.stage[i], self.load.at[i])
        return pltpu.make_async_copy(self.stage[i], self.rows(i, self.z, self.core), self.store.at[i])

    def keep(self, i):
        self.local(i, 0).wait()
        self.local(i, 1).start()

    def arrived(self, i, k, quarter, semaphore):
        ref = self.rows(i, self.source(k), self.core, quarter)
        self.copy(ref, ref, self.ps.at[0], semaphore, self.to_x).wait_recv()
        return ref

    def plane(self, i, k):
        at = 3 * i + k
        ref = self.arrived(i, k, self.rep, self.zr.at[at])
        if k:
            hand = self.copy(ref, ref, self.hs.at[2 * i + k - 1], self.zr.at[at], self.along(3 * self.high))
            pl.when(self.inner == 1)(hand.start)
            self.handed.append(hand)
        self.start(ref, ref, self.ps.at[2 * at], self.pr.at[2 * at], self.to_x)
        self.start(ref, ref, self.ps.at[2 * at + 1], self.pr.at[2 * at + 1], self.to_y)

    def diagonal(self, i, k):
        at = 3 * i + k
        from_x = self.arrived(i, k, self.over_x, self.pr.at[2 * at])
        from_y = self.arrived(i, k, self.over_y, self.pr.at[2 * at + 1])
        if at % 2:
            self.start(from_x, from_x, self.fs.at[at], self.fr.at[at], self.to_y)
        else:
            self.start(from_y, from_y, self.fs.at[at], self.fr.at[at], self.to_x)

    def share(self, i, k):
        self.arrived(i, k, self.across, self.fr.at[3 * i + k])
        ref = self.rows(i, self.source(k), self.core)
        self.start(ref, ref, self.cs.at[4 * i + k + 1], self.cr.at[4 * i + k + 1], self.to_core)

    def shared(self, i):
        for k in range(4):
            ref = self.rows(i, self.source(k - 1) if k else self.z, 1 - self.core)
            self.copy(ref, ref, self.ps.at[0], self.cr.at[4 * i + k], self.to_core).wait_recv()
        self.local(i, 1).wait()

    def steps(self, lag=2):
        items = [(i, k) for i in range(self.n) for k in range(3)]
        for step in range(len(items) + 2 * lag):
            if step < len(items):
                self.plane(*items[step])
            if lag <= step < len(items) + lag:
                self.diagonal(*items[step - lag])
            if 2 * lag <= step:
                self.share(*items[step - 2 * lag])
            yield step

    def finish(self):
        for copy in self.sent:
            copy.wait_send()
        for hand in self.handed:
            pl.when(self.inner == 1)(hand.wait_send)

    @staticmethod
    def scratch(blocks):
        n, dma = len(blocks), pltpu.SemaphoreType.DMA
        sizes = (n, n, 2 * n, 3 * n, 2 * n, 6 * n, 6 * n, 3 * n, 3 * n, 4 * n, 4 * n)
        return [pltpu.VMEM(b.shape, b.dtype) for b in blocks] + [dma((s,)) for s in sizes]


def gather_kernel(n, *refs):
    g = Gather(n, refs[:n], refs[n:2 * n], refs[2 * n:3 * n], *refs[3 * n:])
    g.barrier()
    for i in range(n):
        g.begin(i)
    for i in range(n):
        g.keep(i)
    for _ in g.steps():
        pass
    for i in range(n):
        g.shared(i)
    g.finish()


def gather(blocks, collective_id=0):
    n = len(blocks)
    anywhere = pl.BlockSpec(memory_space=pltpu.HBM)
    return pl.pallas_call(
        functools.partial(gather_kernel, n),
        in_specs=[anywhere] * n,
        out_specs=[anywhere] * n,
        out_shape=[jax.ShapeDtypeStruct((8 * b.shape[0], b.shape[1]), b.dtype) for b in blocks],
        scratch_shapes=Gather.scratch(blocks),
        compiler_params=pltpu.CompilerParams(collective_id=collective_id, has_side_effects=True),
        cost_estimate=pl.CostEstimate(flops=25_000_000_000 * n, bytes_accessed=48 * 2**20, transcendentals=0),
        name="gather",
    )(*blocks)


def solution(mesh):
    def body(x, dy, wg, wu, wd):
        gather_all = functools.partial(lax.all_gather, axis_name="dp", axis=0, tiled=True)
        me = lax.axis_index("dp")
        h0, g2 = x[0], dy[0]
        width = wd.shape[1]
        all_g2, all_a0 = gather_all(g2), gather_all(normed(h0))
        flat = gather([w[n] for n in range(2) for w in (wg, wu, wd)])
        full = flat[:3], flat[3:]
        own = [(*(lax.dynamic_slice_in_dim(w, me * width, width, 1) for w in f[:2]), wd[n]) for n, f in enumerate(full)]
        h0, all_g2, all_a0 = lax.optimization_barrier((h0, all_g2, all_a0))
        h1, a1 = forward(h0, *full[0])
        all_a1 = gather_all(a1)
        g1 = back(h1, g2, *full[1])
        all_g1 = gather_all(g1)
        g0 = back(h0, g1, *full[0])
        all_a1, g0 = lax.optimization_barrier((all_a1, g0))
        upper = weights_back(all_a1, all_g2, *own[1], collective_id=2)
        all_g1, upper = lax.optimization_barrier((all_g1, upper))
        lower = weights_back(all_a0, all_g1, *own[0], collective_id=2)
        return (g0[None], *(jnp.stack(t) for t in zip(lower, upper)))

    rows = P(("rep", "dp"), None, None)
    w = P(None, "dp", None)
    out = P("rep", "dp", None)
    return jax.shard_map(body, mesh=mesh, in_specs=(rows, rows, w, w, w), out_specs=(rows, out, out, out), check_vma=False)
```

time: 1040 us -> 612 us (0.59)
  Pallas kernels: 0 us -> 573 us
  matrix products: 491 us -> 0 us
  waiting for transfers between devices: 471 us -> 0.81 us
  starting transfers between devices: 17.8 us -> 0.34 us
  local copies, waits for them, and re-layouts: 24.4 us -> 13.1 us
    pallas_call x0 -> x6, Pallas kernels: none -> 573 us  [the longest x1 259 us: gather(): pl.pallas_call(functools.partial(gather_kernel, n), in_specs=[anywhere] *...]
    dot_general x22 -> x0, matrix products: 491 us -> none  [dot(): lax.dot_general(a, b, (((ca,), (cb,)), ((), ())), preferred_element_type=...]
    all_gather x10 -> x4, waiting for transfers between devices: 460 us -> 0.06 us  [the longest x2 0.04 us: body(): all_g2, all_a0 = (gather_all(g2), gather_all(normed(h0)))]
    all_to_all x4 -> x0, starting transfers between devices: 17.4 us -> none  [body(): bg, bu = (lax.all_to_all(t, 'dp', 0, 1, tiled=True) for t in (bg, bu))]
  transfers between devices with their start and end apart: 14 -> 4, of which waited for: 10 -> 0; matrix products, arithmetic and copies ran while one was open for 50% -> 2% of each run, Pallas kernels for 0% -> 75%
where the time goes in v2:
time: 612 us; the launch traced here: 611 us
  Pallas kernels  573 us (94%)
  between operations  13.9 us (2%)
  local copies, waits for them, and re-layouts  13.1 us (2%)
  other arithmetic  10.1 us (2%)
    pallas_call x1, Pallas kernels, gather(): pl.pallas_call(functools.partial(gather_kernel, n), in_specs=[anywhere] *...  259 us
    pallas_call x2, Pallas kernels, weights_back(): pl.pallas_call(weights_kernel, grid=(chunks, tokens // block), in_specs=[...  172 us
    pallas_call x2, Pallas kernels, back(): pl.pallas_call(back_kernel, grid=(ff // width,), in_specs=[whole, whole,...  110 us
    pallas_call x1, Pallas kernels, forward(): pl.pallas_call(forward_kernel, grid=(ff // width,), in_specs=[whole, colu...  32.6 us
  transfers between devices with their start and end apart: 4, of which 0 were waited for; matrix products, arithmetic and copies ran while one was open for 2% of the time, Pallas kernels for 75%

profile of v2, /device:TPU:0, one launch (start us, length us, event | category | flops | bytes accessed | tf_op | source)
XLA Modules:
  0.0 611.3 jit_solution(9740828914835863991)
XLA Ops:
  7.2 0.0 all-gather.6.cloned.1.call-start
  7.2 1.5 fusion
  8.7 0.0 copy-start
  8.7 2.7 fusion.1
  11.5 0.0 all-gather.6.cloned.1.call-update
  11.5 0.0 all-gather.12.cloned.1.call-start
  11.5 0.7 all-gather.12.cloned.1.call-update
  12.2 0.0 all-gather.8.cloned.1.call-start
  12.3 0.0 copy-done
  12.3 0.0 copy-start.1
  12.3 1.5 slice_bitcast_fusion.1
  13.8 0.9 copy-done.1
  14.7 0.0 copy-start.2
  14.7 1.5 slice_bitcast_fusion.2
  16.1 0.9 copy-done.2
  17.0 1.5 slice_bitcast_fusion
  18.5 259.0 %gather.1 = (bf16[512,8192]{1,0:T(8,128)(2,1)}, bf16[512,8192]{1,0:T(8,128)(2,1)}, bf16[8192,512]{1,0:T(8,128)(2,1)}, bf16[512,8192]{1,0:T(8,128)(2,1)}, bf16[51...) custom-call(bf16[64,8192]{1,0:T(8,128)(2,1)} %get-tuple-element.55.refs_0_, bf16[64,8192]{1,0:T(8,128)(2,1)} %get-tuple-element.53.refs_1_, ...), custom_call_target="tpu_custom_call" | custom-call | flops 149999992832 | bytes 50331648 | tf_op jit(solution)/shard_map/gather/pallas_call | solution.py:365
  277.5 0.0 all-gather.6.cloned.1.call-done.a_ref
  277.6 0.0 all-gather.12.cloned.1.call-done
  277.6 32.6 %forward.1 = (bf16[1024,512]{1,0:T(8,128)(2,1)}, bf16[1024,512]{1,0:T(8,128)(2,1)}) custom-call(bf16[1024,512]{1,0:T(8,128)(2,1)} %bitcast.24, bf16[512,8192]{1,0:T(8,128)(2,1)} %get-tuple-element.28.wg_ref, bf16[512,8192]{1,0:T(8,128)(2,1)} %get-tuple-element.29.wu_ref, bf16[8192,512]{1,0:T(8,128)(2,1)} %get-tuple-element.30.wd_ref), custom_call_target="tpu_custom_call" | custom-call | flops 25769803776 | bytes 25165824 | tf_op jit(solution)/shard_map/forward/pallas_call | solution.py:68
  310.2 0.0 all-gather.8.cloned.1.call-update
  310.2 0.2 all-gather.10.cloned.1.call-start
  310.4 54.8 %back.2.g_ref = bf16[1024,512]{1,0:T(8,128)(2,1)} custom-call(bf16[1024,512]{1,0:T(8,128)(2,1)} %get-tuple-element.32.h_ref, bf16[1024,512]{1,0:T(8,128)(2,1)} %bitcast.26, bf16[512,8192]{1,0:T(8,128)(2,1)} %get-tuple-element.33.wg_ref, bf16[512,8192]{1,0:T(8,128)(2,1)} %get-tuple-element.34.wu_ref, bf16[8192,512]{1,0:T(8,128)(2,1)} %get-tuple-element.35.wd_ref), custom_call_target="tpu_custom_call" | custom-call | flops 42949672960 | bytes 25165824 | tf_op jit(solution)/shard_map/back/pallas_call | solution.py:108
  365.2 0.0 all-gather.10.cloned.1.call-update
  365.2 3.1 constant_dynamic-slice_fusion.2
  368.3 3.1 constant_dynamic-slice_fusion
  371.4 54.8 %back.3 = bf16[1024,512]{1,0:T(8,128)(2,1)} custom-call(bf16[1024,512]{1,0:T(8,128)(2,1)} %bitcast.25, bf16[1024,512]{1,0:T(8,128)(2,1)} %back.2.g_ref, bf16[512,8192]{1,0:T(8,128)(2,1)} %get-tuple-element.28.wg_ref, bf16[512,8192]{1,0:T(8,128)(2,1)} %get-tuple-element.29.wu_ref, bf16[8192,512]{1,0:T(8,128)(2,1)} %get-tuple-element.30.wd_ref), custom_call_target="tpu_custom_call" | custom-call | flops 42949672960 | bytes 25165824 | tf_op jit(solution)/shard_map/back/pallas_call | solution.py:108
  426.2 0.0 all-gather.8.cloned.1.call-done.a_ref
  426.2 90.5 %weights_back.2 = (bf16[64,8192]{1,0:T(8,128)(2,1)}, bf16[64,8192]{1,0:T(8,128)(2,1)}, bf16[1024,512]{1,0:T(8,128)(2,1)}) custom-call(bf16[8192,512]{1,0:T(8,128)(2,1)} %all-gather.8.cloned.1.call-done.a_ref, bf16[8192,512]{1,0:T(8,128)(2,1)} %bitcast.33, bf16[512,1024]{1,0:T(8,128)(2,1)} %get-tuple-element.59.wg_ref, ...), custom_call_target="tpu_custom_call" | custom-call | flops 51539607552 | bytes 67108864 | tf_op jit(solution)/shard_map/weights_back/pallas_call | solution.py:204
  516.7 0.0 all-gather.10.cloned.1.call-done.g_ref
  516.8 0.0 copy-start.5
  516.8 81.2 %weights_back.3 = (bf16[64,8192]{1,0:T(8,128)(2,1)}, bf16[64,8192]{1,0:T(8,128)(2,1)}, bf16[1024,512]{1,0:T(8,128)(2,1)}) custom-call(bf16[8192,512]{1,0:T(8,128)(2,1)} %all-gather.6.cloned.1.call-done.a_ref, bf16[8192,512]{1,0:T(8,128)(2,1)} %all-gather.10.cloned.1.call-done.g_ref, bf16[512,1024]{1,0:T(8,128)(2,1)} %get-tuple-element.57.wg_ref, ...), custom_call_target="tpu_custom_call" | custom-call | flops 51539607552 | bytes 67108864 | tf_op jit(solution)/shard_map/weights_back/pallas_call | solution.py:204
  598.0 0.0 copy-done.5
  598.0 0.0 copy-start.4
  598.0 0.0 copy-start.7
  598.0 2.9 pad_maximum_fusion.2
  600.9 0.0 copy-done.4
  600.9 0.0 copy-done.7
  600.9 0.0 copy-start.3
  600.9 0.0 copy-start.6
  600.9 1.5 pad_maximum_fusion.1
  602.4 0.0 copy-done.3
  602.4 0.8 copy-done.6
  603.2 1.5 pad_maximum_fusion
  (1 shorter events, 0.0 us)
Async XLA Ops:
  7.2 270.4 %all-gather.6.cloned.1.call-start = ((), (), s32[]{:S(2)}) async-start(), calls=%async_computation | async-start | bytes 9437184 | tf_op jit(solution)/shard_map/all_gather | solution.py:383
  8.7 3.6 copy-start
  11.5 266.1 %all-gather.12.cloned.1.call-start = ((), (), s32[]{:S(2)}) async-start(), calls=%async_computation.3 | async-start | bytes 9437184 | tf_op jit(solution)/shard_map/all_gather | solution.py:383
  12.2 413.9 %all-gather.8.cloned.1.call-start = ((), (), s32[]{:S(2)}) async-start(), calls=%async_computation.1 | async-start | bytes 9437184 | tf_op jit(solution)/shard_map/all_gather | solution.py:389
  12.3 2.4 copy-start.1
  14.7 2.3 copy-start.2
  310.2 206.6 %all-gather.10.cloned.1.call-start = ((), (), s32[]{:S(2)}) async-start(), calls=%async_computation.2 | async-start | bytes 9437184 | tf_op jit(solution)/shard_map/all_gather | solution.py:391
  516.8 81.2 %copy-start.5 = (bf16[1024,512]{1,0:T(8,128)(2,1)S(1)}, bf16[1024,512]{1,0:T(8,128)(2,1)}, u32[]{:S(2)}) copy-start(bf16[1024,512]{1,0:T(8,128)(2,1)} %get-tuple-element.49) | copy-start | bytes 3145732
  598.0 2.9 copy-start.4
  598.0 2.9 copy-start.7
  600.9 1.5 copy-start.3
  600.9 2.3 copy-start.6
Sparse Core Ops, SparseCore 0:
  11.6 149.0 all-gather.5
  162.3 100.1 all-gather.11
  310.3 79.9 all-gather.7
  392.3 123.0 all-gather.9

commit v3 on v2

--- a/solution.py
+++ b/solution.py
@@ -35,46 +35,7 @@
     return (s * up).astype(BF16), (dp * up * (sig + s * (1 - sig))).astype(BF16), (dp * s).astype(BF16)
 
 
-ROWS = 256
-
-
-def forward_kernel(h_ref, wg_ref, wu_ref, wd_ref, out_ref, normed_ref, a_ref, acc_ref):
-    step = pl.program_id(0)
-
-    @pl.when(step == 0)
-    def _():
-        a_ref[...] = normed(h_ref[...])
-        acc_ref[...] = jnp.zeros_like(acc_ref)
-
-    for r in range(0, h_ref.shape[0], ROWS):
-        rows = pl.ds(r, ROWS)
-        a = a_ref[rows, :]
-        gate, up = dot(a, wg_ref[...], 1, 0), dot(a, wu_ref[...], 1, 0)
-        p = (gate * jax.nn.sigmoid(gate) * up).astype(BF16)
-        acc_ref[rows, :] += dot(p, wd_ref[...], 1, 0)
-
-    @pl.when(step == pl.num_programs(0) - 1)
-    def _():
-        h = h_ref[...] + acc_ref[...].astype(BF16)
-        out_ref[...] = h
-        normed_ref[...] = normed(h)
-
-
-def forward(h, wg, wu, wd, width=1024):
-    tokens, d = h.shape
-    ff = wd.shape[0]
-    whole = pl.BlockSpec((tokens, d), lambda k: (0, 0))
-    column = pl.BlockSpec((d, width), lambda k: (0, k))
-    return pl.pallas_call(
-        forward_kernel,
-        grid=(ff // width,),
-        in_specs=[whole, column, column, pl.BlockSpec((width, d), lambda k: (k, 0))],
-        out_specs=[whole, whole],
-        out_shape=[jax.ShapeDtypeStruct(h.shape, BF16)] * 2,
-        scratch_shapes=[pltpu.VMEM((tokens, d), BF16), pltpu.VMEM((tokens, d), F32)],
-        cost_estimate=pl.CostEstimate(flops=6 * tokens * d * ff, bytes_accessed=6 * d * ff, transcendentals=tokens * ff),
-        name="forward",
-    )(h, wg, wu, wd)
+ROWS = 512
 
 
 def back_kernel(h_ref, g_ref, wg_ref, wu_ref, wd_ref, out_ref, a_ref, accg_ref, accu_ref):
@@ -120,27 +81,14 @@
 GROUP = 8
 
 
-def weights_kernel(a_ref, g_ref, wg_ref, wu_ref, wd_ref, bg_ref, bu_ref, bd_ref, accg_ref, accu_ref, accd_ref, stageg_ref, stageu_ref,
-                   kept, sends, receives):
-    chunk, step = pl.program_id(0), pl.program_id(1)
-    chunks, steps = pl.num_programs(0), pl.num_programs(1)
-    tokens, width = a_ref.shape[0], wg_ref.shape[1]
-    height = bg_ref.shape[0]
-    rep, me = lax.axis_index("rep"), lax.axis_index("dp")
-    barrier = pltpu.get_barrier_semaphore()
-
-    @pl.when((chunk == 0) & (step == 0))
-    def _():
-        for j in range(1, GROUP):
-            pl.semaphore_signal(barrier, inc=1, device_id=(rep, lax.rem(me + j, GROUP)), device_id_type=pl.DeviceIdType.MESH)
-
-    @pl.when(step == 0)
+def weights_step(a_ref, g_ref, wg_ref, wu_ref, wd_ref, accg_ref, accu_ref, accd_ref):
+    @pl.when(pl.program_id(1) == 0)
     def _():
         for acc in (accg_ref, accu_ref, accd_ref):
             acc[...] = jnp.zeros_like(acc)
 
     ps, dgs, dus = [], [], []
-    for r in range(0, tokens, ROWS):
+    for r in range(0, a_ref.shape[0], ROWS):
         rows = pl.ds(r, ROWS)
         a, g = a_ref[rows, :], g_ref[rows, :]
         gate, up = dot(a, wg_ref[...], 1, 0), dot(a, wu_ref[...], 1, 0)
@@ -151,36 +99,74 @@
     accu_ref[...] += dot(a_ref[...], dup, 0, 0)
     accd_ref[...] += dot(p, g_ref[...], 0, 0)
 
-    pairs = ((stageg_ref, bg_ref), (stageu_ref, bu_ref))
+
+def upper_kernel(a_ref, g_ref, wg_ref, wu_ref, wd_ref, bg_ref, bu_ref, bd_ref, *accs):
+    weights_step(a_ref, g_ref, wg_ref, wu_ref, wd_ref, *accs)
+
+    @pl.when(pl.program_id(1) == pl.num_programs(1) - 1)
+    def _():
+        for out, acc in zip((bg_ref, bu_ref, bd_ref), accs):
+            out[...] = acc[...].astype(BF16)
+
+
+def lower_kernel(a_ref, g_ref, wg_ref, wu_ref, wd_ref, ready_g, ready_u, bg_ref, bu_ref, bd_ref, cg_ref, cu_ref,
+                 accg_ref, accu_ref, accd_ref, stageg_ref, stageu_ref, kept, sends, receives):
+    chunk, step = pl.program_id(0), pl.program_id(1)
+    chunks, steps = pl.num_programs(0), pl.num_programs(1)
+    width = wg_ref.shape[1]
+    height = bg_ref.shape[0]
+    rep, me = lax.axis_index("rep"), lax.axis_index("dp")
+    barrier = pltpu.get_barrier_semaphore()
+
+    @pl.when((chunk == 0) & (step == 0))
+    def _():
+        for j in range(1, GROUP):
+            pl.semaphore_signal(barrier, inc=1, device_id=(rep, lax.rem(me + j, GROUP)), device_id_type=pl.DeviceIdType.MESH)
+
+    weights_step(a_ref, g_ref, wg_ref, wu_ref, wd_ref, accg_ref, accu_ref, accd_ref)
+
+    def place(c, m):
+        if isinstance(c, int) and c < 0:
+            return ((ready_g, cg_ref), (ready_u, cu_ref))[m], pl.ds(pl.multiple_of(me * chunks * width, chunks * width), chunks * width), 0
+        stage, out = ((stageg_ref, bg_ref), (stageu_ref, bu_ref))[m]
+        return (stage.at[c], out), pl.ds(pl.multiple_of((me * chunks + c) * width, width), width), c + 1
 
     def to_own(c, m):
-        stage, out = pairs[m]
-        columns = pl.ds(pl.multiple_of((me * chunks + c) * width, width), width)
-        return pltpu.make_async_copy(stage.at[c, pl.ds(pl.multiple_of(me * height, height), height)], out.at[:, columns], kept.at[c, m])
+        (source, out), columns, s = place(c, m)
+        return pltpu.make_async_copy(source.at[pl.ds(pl.multiple_of(me * height, height), height)], out.at[:, columns], kept.at[s, m])
 
     def to_peer(c, m, j):
-        stage, out = pairs[m]
-        columns = pl.ds(pl.multiple_of((me * chunks + c) * width, width), width)
+        (source, out), columns, s = place(c, m)
         peer = lax.rem(me + j, GROUP)
         return pltpu.make_async_remote_copy(
-            src_ref=stage.at[c, pl.ds(pl.multiple_of(peer * height, height), height)], dst_ref=out.at[:, columns],
-            send_sem=sends.at[c, m, j - 1], recv_sem=receives.at[c, m, j - 1], device_id=(rep, peer), device_id_type=pl.DeviceIdType.MESH)
-
-    @pl.when((chunk == 0) & (step == steps - 1))
+            src_ref=source.at[pl.ds(pl.multiple_of(peer * height, height), height)], dst_ref=out.at[:, columns],
+            send_sem=sends.at[s, m, j - 1], recv_sem=receives.at[s, m, j - 1], device_id=(rep, peer), device_id_type=pl.DeviceIdType.MESH)
+
+    def spread(c, m):
+        for j in (4, 3, 5, 2, 6, 1, 7):
+            to_peer(c, m, j).start()
+        to_own(c, m).start()
+
+    @pl.when((chunk == 0) & (step == 1))
     def _():
         pl.semaphore_wait(barrier, GROUP - 1)
+        for m in range(2):
+            spread(-1, m)
 
     @pl.when(step == steps - 1)
     def _():
-        for m, acc in ((0, accg_ref), (1, accu_ref)):
-            pairs[m][0][chunk] = acc[...].astype(BF16)
-            for j in (4, 3, 5, 2, 6, 1, 7):
-                to_peer(chunk, m, j).start()
-            to_own(chunk, m).start()
+        for m, stage, acc in ((0, stageg_ref, accg_ref), (1, stageu_ref, accu_ref)):
+            stage[chunk] = acc[...].astype(BF16)
+            spread(chunk, m)
         bd_ref[...] = accd_ref[...].astype(BF16)
 
     @pl.when((chunk == chunks - 1) & (step == steps - 1))
     def _():
+        for m in range(2):
+            to_own(-1, m).wait()
+            for j in range(1, GROUP):
+                to_peer(-1, m, j).wait()
+
         def finish(c, _):
             for m in range(2):
                 to_own(c, m).wait()
@@ -191,29 +177,36 @@
         lax.fori_loop(0, chunks, finish, 0)
 
 
-def weights_back(a, g, wg, wu, wd, collective_id, width=256, block=1024):
+def weights_back(a, g, wg, wu, wd, layer, ready=None, width=256, block=1024):
     tokens, d = a.shape
-    ff = wd.shape[0]
+    ff = wd.shape[1]
     chunks = ff // width
     rows = pl.BlockSpec((block, d), lambda k, t: (t, 0))
-    column = pl.BlockSpec((d, width), lambda k, t: (0, k))
-    down = pl.BlockSpec((width, d), lambda k, t: (k, 0))
+    column = pl.BlockSpec((d, width), lambda k, t: (0, lax.axis_index("dp") * chunks + k))
+    column_out = pl.BlockSpec((d, width), lambda k, t: (0, k))
+    down = pl.BlockSpec((None, width, d), lambda k, t: (layer, k, 0))
+    down_out = pl.BlockSpec((width, d), lambda k, t: (k, 0))
     anywhere = pl.BlockSpec(memory_space=pltpu.HBM)
+    accs = [pltpu.VMEM((d, width), F32), pltpu.VMEM((d, width), F32), pltpu.VMEM((width, d), F32)]
+    half = jax.ShapeDtypeStruct((d, ff), BF16)
+    bd = jax.ShapeDtypeStruct((ff, d), BF16)
+    cost = pl.CostEstimate(flops=12 * tokens * d * ff, bytes_accessed=4 * d * tokens * chunks, transcendentals=tokens * ff)
+    common = dict(grid=(chunks, tokens // block), cost_estimate=cost)
+    if ready is None:
+        return pl.pallas_call(
+            upper_kernel, in_specs=[rows, rows, column, column, down], out_specs=[column_out, column_out, down_out],
+            out_shape=[half, half, bd], scratch_shapes=accs, name="weights_upper", **common)(a, g, wg, wu, wd)
     spread = jax.ShapeDtypeStruct((d // GROUP, ff * GROUP), BF16)
     dma = pltpu.SemaphoreType.DMA
     return pl.pallas_call(
-        weights_kernel,
-        grid=(chunks, tokens // block),
-        in_specs=[rows, rows, column, column, down],
-        out_specs=[anywhere, anywhere, down],
-        out_shape=[spread, spread, jax.ShapeDtypeStruct((ff, d), BF16)],
-        scratch_shapes=[pltpu.VMEM((d, width), F32), pltpu.VMEM((d, width), F32), pltpu.VMEM((width, d), F32),
-                        pltpu.VMEM((chunks, d, width), BF16), pltpu.VMEM((chunks, d, width), BF16),
-                        dma((chunks, 2)), dma((chunks, 2, GROUP - 1)), dma((chunks, 2, GROUP - 1))],
-        compiler_params=pltpu.CompilerParams(collective_id=collective_id, has_side_effects=True),
-        cost_estimate=pl.CostEstimate(flops=12 * tokens * d * ff, bytes_accessed=4 * d * tokens * chunks, transcendentals=tokens * ff),
-        name="weights_back",
-    )(a, g, wg, wu, wd)
+        lower_kernel,
+        in_specs=[rows, rows, column, column, down, anywhere, anywhere],
+        out_specs=[anywhere, anywhere, down_out, anywhere, anywhere],
+        out_shape=[spread, spread, bd, spread, spread],
+        scratch_shapes=accs + [pltpu.VMEM((chunks, d, width), BF16), pltpu.VMEM((chunks, d, width), BF16), dma((chunks + 1, 2)),
+                               dma((chunks + 1, 2, GROUP - 1)), dma((chunks + 1, 2, GROUP - 1))],
+        compiler_params=pltpu.CompilerParams(collective_id=2, has_side_effects=True), name="weights_lower", **common,
+    )(a, g, wg, wu, wd, *ready)
 
 
 MESH = pl.DeviceIdType.MESH
@@ -345,56 +338,103 @@
         return [pltpu.VMEM(b.shape, b.dtype) for b in blocks] + [dma((s,)) for s in sizes]
 
 
-def gather_kernel(n, *refs):
-    g = Gather(n, refs[:n], refs[n:2 * n], refs[2 * n:3 * n], *refs[3 * n:])
+WIDTH = 512
+FIRST_STEP = 14
+
+
+def gather_kernel(h_ref, wg_ref, wu_ref, wd_ref, *refs):
+    n = 6
+    out, (h1_ref, a1_ref) = refs[:n], refs[n:n + 2]
+    a_ref, acc_ref, wgb, wub, wdb, fetched = refs[n + 2:n + 8]
+    scratch = refs[n + 8:]
+    g = Gather(n, [w.at[layer] for layer in range(2) for w in (wg_ref, wu_ref, wd_ref)], out, scratch[:n], *scratch[n:])
     g.barrier()
     for i in range(n):
         g.begin(i)
     for i in range(n):
         g.keep(i)
-    for _ in g.steps():
-        pass
-    for i in range(n):
+    a_ref[...] = normed(h_ref[...])
+    acc_ref[...] = jnp.zeros_like(acc_ref)
+    chunks = out[2].shape[0] // WIDTH
+
+    def fetch(c, slot):
+        units = pl.ds(pl.multiple_of(c * WIDTH, WIDTH), WIDTH)
+        return (pltpu.make_async_copy(out[0].at[:, units], wgb.at[slot], fetched.at[0, slot]),
+                pltpu.make_async_copy(out[1].at[:, units], wub.at[slot], fetched.at[1, slot]),
+                pltpu.make_async_copy(out[2].at[units], wdb.at[slot], fetched.at[2, slot]))
+
+    def chunk(c, _):
+        slot = lax.rem(c, 2)
+
+        @pl.when(c + 1 < chunks)
+        def _():
+            for copy in fetch(c + 1, 1 - slot):
+                copy.start()
+
+        for copy in fetch(c, slot):
+            copy.wait()
+        for r in range(0, h_ref.shape[0], ROWS):
+            rows = pl.ds(r, ROWS)
+            a = a_ref[rows, :]
+            gate, up = dot(a, wgb[slot], 1, 0), dot(a, wub[slot], 1, 0)
+            p = (gate * jax.nn.sigmoid(gate) * up).astype(BF16)
+            acc_ref[rows, :] += dot(p, wdb[slot], 1, 0)
+        return 0
+
+    for step in g.steps():
+        turn, off = divmod(step - FIRST_STEP, 2)
+        if turn < 0 or off:
+            continue
+        if turn == 0:
+            for i in range(3):
+                g.shared(i)
+            for copy in fetch(0, 0):
+                copy.start()
+        lax.fori_loop(turn * chunks // 4, (turn + 1) * chunks // 4, chunk, 0)
+    h = h_ref[...] + acc_ref[...].astype(BF16)
+    h1_ref[...] = h
+    a1_ref[...] = normed(h)
+    for i in range(3, n):
         g.shared(i)
     g.finish()
 
 
-def gather(blocks, collective_id=0):
-    n = len(blocks)
+def gather(h, wg, wu, wd):
+    blocks = [jax.ShapeDtypeStruct(w.shape[1:], w.dtype) for _ in range(2) for w in (wg, wu, wd)]
     anywhere = pl.BlockSpec(memory_space=pltpu.HBM)
+    vmem = pl.BlockSpec(memory_space=pltpu.VMEM)
+    tokens, d = h.shape
     return pl.pallas_call(
-        functools.partial(gather_kernel, n),
-        in_specs=[anywhere] * n,
-        out_specs=[anywhere] * n,
-        out_shape=[jax.ShapeDtypeStruct((8 * b.shape[0], b.shape[1]), b.dtype) for b in blocks],
-        scratch_shapes=Gather.scratch(blocks),
-        compiler_params=pltpu.CompilerParams(collective_id=collective_id, has_side_effects=True),
-        cost_estimate=pl.CostEstimate(flops=25_000_000_000 * n, bytes_accessed=48 * 2**20, transcendentals=0),
+        gather_kernel,
+        in_specs=[vmem] + [anywhere] * 3,
+        out_specs=[anywhere] * 6 + [vmem] * 2,
+        out_shape=[jax.ShapeDtypeStruct((8 * b.shape[0], b.shape[1]), b.dtype) for b in blocks] + [jax.ShapeDtypeStruct(h.shape, BF16)] * 2,
+        scratch_shapes=[pltpu.VMEM((tokens, d), BF16), pltpu.VMEM((tokens, d), F32), pltpu.VMEM((2, d, WIDTH), BF16),
+                        pltpu.VMEM((2, d, WIDTH), BF16), pltpu.VMEM((2, WIDTH, d), BF16), pltpu.SemaphoreType.DMA((3, 2))]
+        + Gather.scratch(blocks),
+        compiler_params=pltpu.CompilerParams(collective_id=0, has_side_effects=True),
+        cost_estimate=pl.CostEstimate(flops=200_000_000_000, bytes_accessed=48 * 2**20, transcendentals=0),
         name="gather",
-    )(*blocks)
+    )(h, wg, wu, wd)
 
 
 def solution(mesh):
     def body(x, dy, wg, wu, wd):
         gather_all = functools.partial(lax.all_gather, axis_name="dp", axis=0, tiled=True)
-        me = lax.axis_index("dp")
         h0, g2 = x[0], dy[0]
-        width = wd.shape[1]
         all_g2, all_a0 = gather_all(g2), gather_all(normed(h0))
-        flat = gather([w[n] for n in range(2) for w in (wg, wu, wd)])
-        full = flat[:3], flat[3:]
-        own = [(*(lax.dynamic_slice_in_dim(w, me * width, width, 1) for w in f[:2]), wd[n]) for n, f in enumerate(full)]
-        h0, all_g2, all_a0 = lax.optimization_barrier((h0, all_g2, all_a0))
-        h1, a1 = forward(h0, *full[0])
+        *flat, h1, a1 = gather(h0, wg, wu, wd)
+        lower, upper = flat[:3], flat[3:]
+        h1, all_g2, all_a0 = lax.optimization_barrier((h1, all_g2, all_a0))
         all_a1 = gather_all(a1)
-        g1 = back(h1, g2, *full[1])
+        g1 = back(h1, g2, *upper)
         all_g1 = gather_all(g1)
-        g0 = back(h0, g1, *full[0])
+        g0 = back(h0, g1, *lower)
         all_a1, g0 = lax.optimization_barrier((all_a1, g0))
-        upper = weights_back(all_a1, all_g2, *own[1], collective_id=2)
-        all_g1, upper = lax.optimization_barrier((all_g1, upper))
-        lower = weights_back(all_a0, all_g1, *own[0], collective_id=2)
-        return (g0[None], *(jnp.stack(t) for t in zip(lower, upper)))
+        bg1, bu1, bd1 = weights_back(all_a1, all_g2, *upper[:2], wd, 1, width=512)
+        all_g1, bg1, bu1, bd1 = lax.optimization_barrier((all_g1, bg1, bu1, bd1))
+        bg0, bu0, bd0, bg1, bu1 = weights_back(all_a0, all_g1, *lower[:2], wd, 0, ready=(bg1, bu1))
+        return (g0[None], *(jnp.stack(t) for t in ((bg0, bg1), (bu0, bu1), (bd0, bd1))))
 
     rows = P(("rep", "dp"), None, None)
     w = P(None, "dp", None)

time: 612 us -> 560 us (0.915)
  Pallas kernels: 573 us -> 535 us
  local copies, waits for them, and re-layouts: 13.1 us -> 0.02 us
    pallas_call x4 -> x3, Pallas kernels: 463 us -> 428 us  [the longest x1 263 us: gather(): pl.pallas_call(gather_kernel, in_specs=[vmem] + [anywhere] * 3, out_specs...]
    dynamic_slice x2 -> x0, local copies, waits for them, and re-layouts: 6.16 us -> none  [body(): lax.dynamic_slice_in_dim(w, me * width, width, 1)]
  transfers between devices with their start and end apart: 4 -> 4, of which waited for: 0 -> 0; matrix products, arithmetic and copies ran while one was open for 2% -> 0% of each run, Pallas kernels for 75% -> 78%
where the time goes in v3:
time: 560 us; the launch traced here: 559 us
  Pallas kernels  535 us (96%)
  between operations  13.9 us (2%)
  other arithmetic  9.25 us (2%)
    pallas_call x1, Pallas kernels, gather(): pl.pallas_call(gather_kernel, in_specs=[vmem] + [anywhere] * 3, out_specs...  263 us
    pallas_call x2, Pallas kernels, back(): pl.pallas_call(back_kernel, grid=(ff // width,), in_specs=[whole, whole,...  107 us
    pallas_call x1, Pallas kernels, weights_back(): pl.pallas_call(lower_kernel, in_specs=[rows, rows, column, column, down,...  96.4 us
    pallas_call x1, Pallas kernels, weights_back(): pl.pallas_call(upper_kernel, in_specs=[rows, rows, column, column, down],...  68.9 us
  transfers between devices with their start and end apart: 4, of which 0 were waited for; matrix products, arithmetic and copies ran while one was open for 0% of the time, Pallas kernels for 78%

profile of v3, /device:TPU:0, one launch (start us, length us, event | category | flops | bytes accessed | tf_op | source)
XLA Modules:
  0.0 559.3 jit_solution(17376683872878244308)
XLA Ops:
  7.2 0.0 all-gather.8.cloned.1.call-start
  7.2 1.5 fusion
  8.7 2.5 fusion.1
  11.2 0.0 all-gather.8.cloned.1.call-update
  11.2 0.0 all-gather.12.cloned.1.call-start
  11.3 0.7 all-gather.12.cloned.1.call-update
  12.0 0.0 all-gather.6.cloned.1.call-start
  12.0 262.5 %gather.1 = (bf16[512,8192]{1,0:T(8,128)(2,1)}, bf16[512,8192]{1,0:T(8,128)(2,1)}, bf16[8192,512]{1,0:T(8,128)(2,1)}, bf16[512,8192]{1,0:T(8,128)(2,1)}, bf16[51...) custom-call(bf16[1024,512]{1,0:T(8,128)(2,1)} %bitcast.12, ...), custom_call_target="tpu_custom_call" | custom-call | flops 199999995904 | bytes 50331648 | tf_op jit(solution)/shard_map/gather/pallas_call | solution.py:407
  274.6 0.0 all-gather.6.cloned.1.call-update
  274.6 0.2 all-gather.10.cloned.1.call-start
  274.8 0.0 all-gather.8.cloned.1.call-done.a_ref
  274.8 0.0 all-gather.12.cloned.1.call-done
  274.9 53.5 %back.2.g_ref = bf16[1024,512]{1,0:T(8,128)(2,1)} custom-call(bf16[1024,512]{1,0:T(8,128)(2,1)} %get-tuple-element.31.h_ref, bf16[1024,512]{1,0:T(8,128)(2,1)} %bitcast.14, bf16[512,8192]{1,0:T(8,128)(2,1)} %get-tuple-element.32.wg_ref, bf16[512,8192]{1,0:T(8,128)(2,1)} %get-tuple-element.33.wu_ref, bf16[8192,512]{1,0:T(8,128)(2,1)} %get-tuple-element.34.wd_ref), custom_call_target="tpu_custom_call" | custom-call | flops 42949672960 | bytes 25165824 | tf_op jit(solution)/shard_map/back/pallas_call | solution.py:69
  328.3 0.0 all-gather.10.cloned.1.call-update
  328.4 53.7 %back.3 = bf16[1024,512]{1,0:T(8,128)(2,1)} custom-call(bf16[1024,512]{1,0:T(8,128)(2,1)} %bitcast.13, bf16[1024,512]{1,0:T(8,128)(2,1)} %back.2.g_ref, bf16[512,8192]{1,0:T(8,128)(2,1)} %get-tuple-element.35.wg_ref, bf16[512,8192]{1,0:T(8,128)(2,1)} %get-tuple-element.36.wu_ref, bf16[8192,512]{1,0:T(8,128)(2,1)} %get-tuple-element.37.wd_ref), custom_call_target="tpu_custom_call" | custom-call | flops 42949672960 | bytes 25165824 | tf_op jit(solution)/shard_map/back/pallas_call | solution.py:69
  382.0 0.0 all-gather.6.cloned.1.call-done.a_ref
  382.0 68.9 %weights_upper.1 = (bf16[512,1024]{1,0:T(8,128)(2,1)}, bf16[512,1024]{1,0:T(8,128)(2,1)}, bf16[1024,512]{1,0:T(8,128)(2,1)}) custom-call(bf16[8192,512]{1,0:T(8,128)(2,1)} %all-gather.6.cloned.1.call-done.a_ref, bf16[8192,512]{1,0:T(8,128)(2,1)} %bitcast.21, bf16[512,8192]{1,0:T(8,128)(2,1)} %get-tuple-element.32.wg_ref, ...), custom_call_target="tpu_custom_call" | custom-call | flops 51539607552 | bytes 33554432 | tf_op jit(solution)/shard_map/weights_upper/pallas_call | solution.py:196
  451.0 0.0 all-gather.10.cloned.1.call-done.g_ref
  451.0 0.0 copy-start
  451.0 96.4 %weights_lower.1 = (bf16[64,8192]{1,0:T(8,128)(2,1)}, bf16[64,8192]{1,0:T(8,128)(2,1)}, bf16[1024,512]{1,0:T(8,128)(2,1)}, bf16[64,8192]{1,0:T(8,128)(2,1)}, bf16[64,8192]{1,0:T(8,128)(2,1)}) custom-call(bf16[8192,512]{1,0:T(8,128)(2,1)} %all-gather.8.cloned.1.call-done.a_ref, bf16[8192,512]{1,0:T(8,128)(2,1)} %all-gather.10.cloned.1.call-done.g_ref, ...), custom_call_target="tpu_custom_call" | custom-call | flops 51539607552 | bytes 67108864 | tf_op jit(solution)/shard_map/weights_lower/pallas_call | solution.py:201
  547.4 0.0 copy-done
  547.4 0.0 copy-start.1
  547.4 0.0 copy-start.2
  547.5 0.0 copy-start.3
  547.5 0.0 copy-start.4
  547.5 2.9 pad_maximum_fusion.2
  550.4 0.0 copy-done.1
  550.4 0.0 copy-done.2
  550.4 0.0 copy-done.3
  550.4 0.0 copy-done.4
  550.4 2.4 pad_maximum_fusion
  (1 shorter events, 0.0 us)
Async XLA Ops:
  7.2 267.7 %all-gather.8.cloned.1.call-start = ((), (), s32[]{:S(2)}) async-start(), calls=%async_computation.1 | async-start | bytes 9437184 | tf_op jit(solution)/shard_map/all_gather | solution.py:425
  11.2 263.6 %all-gather.12.cloned.1.call-start = ((), (), s32[]{:S(2)}) async-start(), calls=%async_computation.3 | async-start | bytes 9437184 | tf_op jit(solution)/shard_map/all_gather | solution.py:425
  12.0 370.1 %all-gather.6.cloned.1.call-start = ((), (), s32[]{:S(2)}) async-start(), calls=%async_computation | async-start | bytes 9437184 | tf_op jit(solution)/shard_map/all_gather | solution.py:429
  274.6 176.4 %all-gather.10.cloned.1.call-start = ((), (), s32[]{:S(2)}) async-start(), calls=%async_computation.2 | async-start | bytes 9437184 | tf_op jit(solution)/shard_map/all_gather | solution.py:431
  451.0 96.4 %copy-start = (bf16[1024,512]{1,0:T(8,128)(2,1)S(1)}, bf16[1024,512]{1,0:T(8,128)(2,1)}, u32[]{:S(2)}) copy-start(bf16[1024,512]{1,0:T(8,128)(2,1)} %get-tuple-element.53) | copy-start | bytes 3145732
  547.4 2.9 copy-start.1
  547.4 2.9 copy-start.2
  547.5 2.9 copy-start.3
  547.5 2.9 copy-start.4
Sparse Core Ops, SparseCore 0:
  11.4 144.2 all-gather.7
  157.3 100.1 all-gather.11
  274.7 80.5 all-gather.5
  357.3 80.3 all-gather.9

commit v4 on v3

--- a/solution.py
+++ b/solution.py
@@ -338,22 +338,77 @@
         return [pltpu.VMEM(b.shape, b.dtype) for b in blocks] + [dma((s,)) for s in sizes]
 
 
+class Line:
+    PARTS = 2
+
+    def __init__(self, g, own, out, kept, zs, zr, hs, cs, cr):
+        self.g, self.own, self.out, self.kept = g, own, out, kept
+        self.zs, self.zr, self.hs, self.cs, self.cr = zs, zr, hs, cs, cr
+        self.size = own.shape[0] // self.PARTS
+
+    def piece(self, z, core, part):
+        return self.out.at[pl.ds(pl.multiple_of((z * 2 + core) * self.own.shape[0] + part * self.size, self.size), self.size)]
+
+    def local(self, part):
+        g = self.g
+        return pltpu.make_async_copy(self.own.at[pl.ds(part * self.size, self.size)], self.piece(g.z, g.core, part), self.kept.at[part])
+
+    def begin(self):
+        g = self.g
+        outward = g.inner * (3 * g.z - 3) + (1 - g.inner) * (2 - g.z // 3)
+        for part in range(self.PARTS):
+            mine, there = self.own.at[pl.ds(part * self.size, self.size)], self.piece(g.z, g.core, part)
+            g.start(mine, there, self.zs.at[part, 0], self.zr.at[part, g.inner], g.along(1 + lax.rem(g.z, 2)))
+            g.start(mine, there, self.zs.at[part, 1], self.zr.at[part, 2 * (1 - g.inner)], g.along(outward))
+            g.start(mine, there, self.cs.at[part, 3], self.cr.at[part, 3], g.to_core)
+            self.local(part).start()
+
+    def step(self, part, k):
+        g = self.g
+        ref = self.piece(g.source(k), g.core, part)
+        g.copy(ref, ref, self.zs.at[part, 0], self.zr.at[part, k], g.to_core).wait_recv()
+        if k:
+            hand = g.copy(ref, ref, self.hs.at[part, k - 1], self.zr.at[part, k], g.along(3 * g.high))
+            pl.when(g.inner == 1)(hand.start)
+            g.handed.append(hand)
+        g.start(ref, ref, self.cs.at[part, k], self.cr.at[part, k], g.to_core)
+
+    def steps(self):
+        return [(self, part, k) for part in range(self.PARTS) for k in range(3)]
+
+    def finish(self):
+        g = self.g
+        for part in range(self.PARTS):
+            for k in range(4):
+                ref = self.piece(g.source(k) if k < 3 else g.z, 1 - g.core, part)
+                g.copy(ref, ref, self.zs.at[part, 0], self.cr.at[part, k], g.to_core).wait_recv()
+            self.local(part).wait()
+
+    @classmethod
+    def scratch(cls):
+        return [pltpu.SemaphoreType.DMA(s) for s in ((cls.PARTS,), (cls.PARTS, 2), (cls.PARTS, 3), (cls.PARTS, 2), (cls.PARTS, 4), (cls.PARTS, 4))]
+
+
 WIDTH = 512
-FIRST_STEP = 14
-
-
-def gather_kernel(h_ref, wg_ref, wu_ref, wd_ref, *refs):
+TURNS = (14, 16, 18, 20)
+FIRST_LINE_STEP = 10
+
+
+def gather_kernel(h_ref, g_ref, wg_ref, wu_ref, wd_ref, *refs):
     n = 6
-    out, (h1_ref, a1_ref) = refs[:n], refs[n:n + 2]
-    a_ref, acc_ref, wgb, wub, wdb, fetched = refs[n + 2:n + 8]
-    scratch = refs[n + 8:]
+    out, (h1_ref, a1_ref, allg_ref, alla_ref) = refs[:n], refs[n:n + 4]
+    a0_ref, acc_ref, wgb, wub, wdb, fetched = refs[n + 4:n + 10]
+    lines, scratch = refs[n + 10:n + 22], refs[n + 22:]
     g = Gather(n, [w.at[layer] for layer in range(2) for w in (wg_ref, wu_ref, wd_ref)], out, scratch[:n], *scratch[n:])
+    lines = [Line(g, g_ref, allg_ref, *lines[:6]), Line(g, a0_ref, alla_ref, *lines[6:])]
+    a0_ref[...] = normed(h_ref[...])
     g.barrier()
     for i in range(n):
         g.begin(i)
+    for line in lines:
+        line.begin()
     for i in range(n):
         g.keep(i)
-    a_ref[...] = normed(h_ref[...])
     acc_ref[...] = jnp.zeros_like(acc_ref)
     chunks = out[2].shape[0] // WIDTH
 
@@ -375,57 +430,61 @@
             copy.wait()
         for r in range(0, h_ref.shape[0], ROWS):
             rows = pl.ds(r, ROWS)
-            a = a_ref[rows, :]
+            a = a0_ref[rows, :]
             gate, up = dot(a, wgb[slot], 1, 0), dot(a, wub[slot], 1, 0)
             p = (gate * jax.nn.sigmoid(gate) * up).astype(BF16)
             acc_ref[rows, :] += dot(p, wdb[slot], 1, 0)
         return 0
 
+    waiting = [step for line in lines for step in line.steps()]
     for step in g.steps():
-        turn, off = divmod(step - FIRST_STEP, 2)
-        if turn < 0 or off:
-            continue
-        if turn == 0:
-            for i in range(3):
-                g.shared(i)
-            for copy in fetch(0, 0):
-                copy.start()
-        lax.fori_loop(turn * chunks // 4, (turn + 1) * chunks // 4, chunk, 0)
+        if step in TURNS:
+            turn = TURNS.index(step)
+            if turn == 0:
+                for i in range(3):
+                    g.shared(i)
+                for copy in fetch(0, 0):
+                    copy.start()
+            lax.fori_loop(turn * chunks // len(TURNS), (turn + 1) * chunks // len(TURNS), chunk, 0)
+        if step >= FIRST_LINE_STEP and waiting:
+            line, part, k = waiting.pop(0)
+            line.step(part, k)
     h = h_ref[...] + acc_ref[...].astype(BF16)
     h1_ref[...] = h
     a1_ref[...] = normed(h)
     for i in range(3, n):
         g.shared(i)
+    for line in lines:
+        line.finish()
     g.finish()
 
 
-def gather(h, wg, wu, wd):
+def gather(h, dy, wg, wu, wd):
     blocks = [jax.ShapeDtypeStruct(w.shape[1:], w.dtype) for _ in range(2) for w in (wg, wu, wd)]
     anywhere = pl.BlockSpec(memory_space=pltpu.HBM)
     vmem = pl.BlockSpec(memory_space=pltpu.VMEM)
     tokens, d = h.shape
     return pl.pallas_call(
         gather_kernel,
-        in_specs=[vmem] + [anywhere] * 3,
-        out_specs=[anywhere] * 6 + [vmem] * 2,
-        out_shape=[jax.ShapeDtypeStruct((8 * b.shape[0], b.shape[1]), b.dtype) for b in blocks] + [jax.ShapeDtypeStruct(h.shape, BF16)] * 2,
+        in_specs=[vmem] * 2 + [anywhere] * 3,
+        out_specs=[anywhere] * 6 + [vmem] * 2 + [anywhere] * 2,
+        out_shape=[jax.ShapeDtypeStruct((8 * b.shape[0], b.shape[1]), b.dtype) for b in blocks] + [jax.ShapeDtypeStruct(h.shape, BF16)] * 2
+        + [jax.ShapeDtypeStruct((8 * tokens, d), BF16)] * 2,
         scratch_shapes=[pltpu.VMEM((tokens, d), BF16), pltpu.VMEM((tokens, d), F32), pltpu.VMEM((2, d, WIDTH), BF16),
                         pltpu.VMEM((2, d, WIDTH), BF16), pltpu.VMEM((2, WIDTH, d), BF16), pltpu.SemaphoreType.DMA((3, 2))]
-        + Gather.scratch(blocks),
+        + Line.scratch() + Line.scratch() + Gather.scratch(blocks),
         compiler_params=pltpu.CompilerParams(collective_id=0, has_side_effects=True),
         cost_estimate=pl.CostEstimate(flops=200_000_000_000, bytes_accessed=48 * 2**20, transcendentals=0),
         name="gather",
-    )(h, wg, wu, wd)
+    )(h, dy, wg, wu, wd)
 
 
 def solution(mesh):
     def body(x, dy, wg, wu, wd):
         gather_all = functools.partial(lax.all_gather, axis_name="dp", axis=0, tiled=True)
         h0, g2 = x[0], dy[0]
-        all_g2, all_a0 = gather_all(g2), gather_all(normed(h0))
-        *flat, h1, a1 = gather(h0, wg, wu, wd)
+        *flat, h1, a1, all_g2, all_a0 = gather(h0, g2, wg, wu, wd)
         lower, upper = flat[:3], flat[3:]
-        h1, all_g2, all_a0 = lax.optimization_barrier((h1, all_g2, all_a0))
         all_a1 = gather_all(a1)
         g1 = back(h1, g2, *upper)
         all_g1 = gather_all(g1)

time: 560 us -> 549 us (0.980)
  Pallas kernels: 535 us -> 529 us
    pallas_call x1, Pallas kernels: 263 us -> 255 us  [gather(): pl.pallas_call(gather_kernel, in_specs=[vmem] * 2 + [anywhere] * 3, out_s...]
  transfers between devices with their start and end apart: 4 -> 2, of which waited for: 0 -> 0; matrix products, arithmetic and copies ran while one was open for 0% -> 0% of each run, Pallas kernels for 78% -> 32%
where the time goes in v4:
time: 549 us
  Pallas kernels  529 us (96%)
  between operations  14.1 us (3%)
    pallas_call x1, Pallas kernels, gather(): pl.pallas_call(gather_kernel, in_specs=[vmem] * 2 + [anywhere] * 3, out_s...  255 us
    pallas_call x2, Pallas kernels, back(): pl.pallas_call(back_kernel, grid=(ff // width,), in_specs=[whole, whole,...  107 us
    pallas_call x1, Pallas kernels, weights_back(): pl.pallas_call(lower_kernel, in_specs=[rows, rows, column, column, down,...  98.4 us
    pallas_call x1, Pallas kernels, weights_back(): pl.pallas_call(upper_kernel, in_specs=[rows, rows, column, column, down],...  68.9 us
  transfers between devices with their start and end apart: 2, of which 0 were waited for; matrix products, arithmetic and copies ran while one was open for 0% of the time, Pallas kernels for 32%

profile of v4, /device:TPU:0, one launch (start us, length us, event | category | flops | bytes accessed | tf_op | source)
XLA Modules:
  0.0 548.8 jit_solution(14206492373017173560)
XLA Ops:
  7.2 0.0 all-gather.3.cloned.1.call-start
  7.2 254.7 %gather.1 = (bf16[512,8192]{1,0:T(8,128)(2,1)}, bf16[512,8192]{1,0:T(8,128)(2,1)}, bf16[8192,512]{1,0:T(8,128)(2,1)}, bf16[512,8192]{1,0:T(8,128)(2,1)}, bf16[51...) custom-call(bf16[1024,512]{1,0:T(8,128)(2,1)} %bitcast.17, ...), custom_call_target="tpu_custom_call" | custom-call | flops 199999995904 | bytes 50331648 | tf_op jit(solution)/shard_map/gather/pallas_call | solution.py:467
  261.9 0.0 all-gather.3.cloned.1.call-update
  261.9 0.2 all-gather.5.cloned.1.call-start
  262.2 53.5 %back.2.g_ref = bf16[1024,512]{1,0:T(8,128)(2,1)} custom-call(bf16[1024,512]{1,0:T(8,128)(2,1)} %get-tuple-element.29.h_ref, bf16[1024,512]{1,0:T(8,128)(2,1)} %bitcast.16, bf16[512,8192]{1,0:T(8,128)(2,1)} %get-tuple-element.30.wg_ref, bf16[512,8192]{1,0:T(8,128)(2,1)} %get-tuple-element.31.wu_ref, bf16[8192,512]{1,0:T(8,128)(2,1)} %get-tuple-element.32.wd_ref), custom_call_target="tpu_custom_call" | custom-call | flops 42949672960 | bytes 25165824 | tf_op jit(solution)/shard_map/back/pallas_call | solution.py:69
  315.6 0.0 all-gather.5.cloned.1.call-update
  315.6 53.7 %back.3 = bf16[1024,512]{1,0:T(8,128)(2,1)} custom-call(bf16[1024,512]{1,0:T(8,128)(2,1)} %bitcast.18, bf16[1024,512]{1,0:T(8,128)(2,1)} %back.2.g_ref, bf16[512,8192]{1,0:T(8,128)(2,1)} %get-tuple-element.33.wg_ref, bf16[512,8192]{1,0:T(8,128)(2,1)} %get-tuple-element.34.wu_ref, bf16[8192,512]{1,0:T(8,128)(2,1)} %get-tuple-element.35.wd_ref), custom_call_target="tpu_custom_call" | custom-call | flops 42949672960 | bytes 25165824 | tf_op jit(solution)/shard_map/back/pallas_call | solution.py:69
  369.3 0.0 all-gather.3.cloned.1.call-done.a_ref
  369.3 68.9 %weights_upper.1 = (bf16[512,1024]{1,0:T(8,128)(2,1)}, bf16[512,1024]{1,0:T(8,128)(2,1)}, bf16[1024,512]{1,0:T(8,128)(2,1)}) custom-call(bf16[8192,512]{1,0:T(8,128)(2,1)} %all-gather.3.cloned.1.call-done.a_ref, bf16[8192,512]{1,0:T(8,128)(2,1)} %get-tuple-element.39.g_ref, bf16[512,8192]{1,0:T(8,128)(2,1)} %get-tuple-element.30.wg_ref, ...), custom_call_target="tpu_custom_call" | custom-call | flops 51539607552 | bytes 33554432 | tf_op jit(solution)/shard_map/weights_upper/pallas_call | solution.py:196
  438.2 0.0 all-gather.5.cloned.1.call-done.g_ref
  438.2 0.0 copy-start
  438.2 98.4 %weights_lower.1 = (bf16[64,8192]{1,0:T(8,128)(2,1)}, bf16[64,8192]{1,0:T(8,128)(2,1)}, bf16[1024,512]{1,0:T(8,128)(2,1)}, bf16[64,8192]{1,0:T(8,128)(2,1)}, bf16[64,8192]{1,0:T(8,128)(2,1)}) custom-call(bf16[8192,512]{1,0:T(8,128)(2,1)} %get-tuple-element.37.a_ref, bf16[8192,512]{1,0:T(8,128)(2,1)} %all-gather.5.cloned.1.call-done.g_ref, ...), custom_call_target="tpu_custom_call" | custom-call | flops 51539607552 | bytes 67108864 | tf_op jit(solution)/shard_map/weights_lower/pallas_call | solution.py:201
  536.6 0.0 copy-done
  536.6 0.0 copy-start.1
  536.7 0.0 copy-start.2
  536.7 0.0 copy-start.3
  536.7 0.0 copy-start.4
  536.7 2.9 pad_maximum_fusion.2
  539.6 0.0 copy-done.1
  539.6 0.0 copy-done.2
  539.6 0.0 copy-done.3
  539.6 0.0 copy-done.4
  539.6 2.4 pad_maximum_fusion
Async XLA Ops:
  7.2 362.2 %all-gather.3.cloned.1.call-start = ((), (), s32[]{:S(2)}) async-start(), calls=%async_computation | async-start | bytes 9437184 | tf_op jit(solution)/shard_map/all_gather | solution.py:488
  261.9 176.3 %all-gather.5.cloned.1.call-start = ((), (), s32[]{:S(2)}) async-start(), calls=%async_computation.1 | async-start | bytes 9437184 | tf_op jit(solution)/shard_map/all_gather | solution.py:490
  438.2 98.4 %copy-start = (bf16[1024,512]{1,0:T(8,128)(2,1)S(1)}, bf16[1024,512]{1,0:T(8,128)(2,1)}, u32[]{:S(2)}) copy-start(bf16[1024,512]{1,0:T(8,128)(2,1)} %get-tuple-element.51) | copy-start | bytes 3145732
  536.6 2.9 copy-start.1
  536.7 2.9 copy-start.2
  536.7 2.9 copy-start.3
  536.7 2.9 copy-start.4
Sparse Core Ops, SparseCore 0:
  262.0 79.8 all-gather.2
  344.1 80.3 all-gather.4
